TPU v7x, 32 devices: a whole 2x2x4 slice. The times are simulated.
32 devices in a mesh: rows: 8 (over z, x), cols: 4 (over y, core).
Axes of the slice: x: 2, y: 2, z: 4, core: 2. Of those that a mesh axis runs over, the one named last changes fastest.
Arguments:
- source: float32 [1024, 32768], P('rows', 'cols'), may hold values from -6 to 6
- low_row: int32 [1024], replicated, may hold values from 0 to 1022, as said below
- weight_low: float32 [1024], replicated, may hold values from 0 to 1
Outputs:
- mercator: float32 [1024, 32768], P('rows', 'cols')
- level1: float32 [512, 16384], P('rows', 'cols')
- level2: float32 [256, 8192], P('rows', 'cols')
- level3: float32 [128, 4096], P(('rows', 'cols'))
- level4: float32 [64, 2048], P(('rows', 'cols'))
Inputs may be any that keep to these rules, and one draw needn't show every extreme that they name: With t = 68 degrees in radians, E = ln tan(pi/4 + t/2), y = E * (1 - (2m + 1) / 2048) and lat = 2 atan(exp(y)) - pi/2, the base row of Mercator row m is floor((t - lat) / t * 1024 - 0.5) clipped to the range; low_row[m] differs from it by at most 2 and is then clipped to the range.
All inputs are finite; a program needn't handle non-finite values.
Results may differ from a plain program's by a relative error of at most 0.00007.
Values sent between devices are 32-bit elements; how exact they have to be, the bound alone decides.
A program may use at most 128 MiB of HBM per device.

v0:
```python
import functools
import math

import jax
import jax.numpy as jnp
import numpy as np
from jax import lax
from jax.experimental import pallas as pl
from jax.experimental.pallas import tpu as pltpu
from jax.sharding import PartitionSpec as P

CHUNK = 8
SPLIT = 2
STEP = 2048
JITTER = 2
MESH = pl.DeviceIdType.MESH


def windows(total, parts):
    top = 68.0 * math.pi / 180.0
    edge = math.log(math.tan(math.pi / 4 + top / 2))
    m = np.arange(total, dtype=np.float64)
    y = edge * (1.0 - (2.0 * m + 1.0) / (2.0 * total))
    lat = 2.0 * np.arctan(np.exp(y)) - math.pi / 2
    pos = (top - lat) / top * total - 0.5
    slack = 0.01 * total / 1024
    first = np.clip(np.floor(pos - slack) - JITTER, 0, total - 2).astype(int)
    last = np.clip(np.floor(pos + slack) + JITTER, 0, total - 2).astype(int) + 1
    block = total // parts
    out = []
    for r in range(parts):
        low = int(first[r * block : (r + 1) * block].min())
        high = int(last[r * block : (r + 1) * block].max()) + 1
        low = low // CHUNK * CHUNK
        high = -(-high // CHUNK) * CHUNK
        assert high <= (r + 1) * block
        out.append((low, high))
    return out


def flows(total, parts):
    block = total // parts
    found = {}
    for d, (low, high) in enumerate(windows(total, parts)):
        for s in range(low // block, d):
            a, b = max(low, s * block), min(high, (s + 1) * block)
            if b > a:
                found[s, d] = ((a - s * block) // CHUNK, (b - a) // CHUNK)
    return found


def units(total, parts):
    return {k: (a * SPLIT, n * SPLIT) for k, (a, n) in flows(total, parts).items()}


def table(index, values):
    out = jnp.int32(values[0])
    for i in range(1, len(values)):
        if values[i] != values[i - 1]:
            out = jnp.where(index >= i, jnp.int32(values[i]), out)
    return out


def relays(total, parts):
    moves = units(total, parts)
    pairs = parts // 2
    if max((d - s for s, d in moves), default=0) > 2 or parts % 2:
        return {}
    plan, taken, before = {}, set(), {}
    for parity in (0, 1):
        flow = [(2 * z - parity, 2 * z - parity + 1) for z in range(pairs)]
        load = [moves.get(k, (0, 0))[1] for k in flow]
        goal = [sum(load) // pairs + (z < sum(load) % pairs) for z in range(pairs)]
        across = 0
        for z in range(pairs - 1):
            across += load[z] - goal[z]
            key = flow[z] if across > 0 else flow[z + 1]
            relay = key[1] + (2 if across > 0 else -2)
            used = before.get(key, 0)
            n = min(abs(across), moves.get(key, (0, 0))[1] - used)
            if n <= 0 or relay in taken or relay == key[0] or (parity and across > 0):
                continue
            plan[key + (relay,)] = (used, n)
            before[key] = used + n
            taken.add(relay)
    return plan


def exchange_kernel(total, parts, source_ref, recv_ref, held, send_sem, recv_sem, held_sem):
    me = lax.axis_index("rows")
    moves = units(total, parts)
    wins = windows(total, parts)
    plan = relays(total, parts)
    block = total // parts
    barrier = pltpu.get_barrier_semaphore()

    @pl.loop(1, parts)
    def _(i):
        pl.semaphore_signal(
            barrier, inc=1, device_id={"rows": lax.rem(me + i, parts)}, device_id_type=MESH
        )

    pl.semaphore_wait(barrier, parts - 1)

    piece = source_ref.shape[1] // SPLIT

    def chunk_of(ref, at):
        rows = pl.ds(pl.multiple_of(lax.div(at, SPLIT) * CHUNK, CHUNK), CHUNK)
        columns = pl.ds(pl.multiple_of(lax.rem(at, SPLIT) * piece, piece), piece)
        return ref.at[rows, columns]

    def held_at(i):
        return held.at[pl.ds(pl.multiple_of(i * CHUNK, CHUNK), CHUNK)]

    def copy(src, dst, at, landed, target):
        return pltpu.make_async_remote_copy(
            src_ref=src,
            dst_ref=dst,
            send_sem=send_sem.at[at],
            recv_sem=landed,
            device_id={"rows": target},
            device_id_type=MESH,
        )

    def slot_of(s, d):
        return (s * block - wins[d][0]) // CHUNK * SPLIT + moves[s, d][0]

    base = jnp.int32(0)
    by_source = {(s, r - s): (moves[s, d][0] + a, n) for (s, d, r), (a, n) in plan.items()}
    for shift in sorted({k[1] for k in by_source}):
        mine = [by_source.get((s, shift), (0, 0)) for s in range(parts)]
        first = table(me, [v[0] for v in mine])
        count = table(me, [v[1] for v in mine])
        start = base
        target = lax.rem(me + shift + parts, parts)

        @pl.loop(0, count)
        def _(i):
            copy(
                chunk_of(source_ref, first + i),
                held_at(i),
                start + i,
                held_sem.at[i],
                target,
            ).start()

        base = base + count

    for delta in sorted({d - s for s, d in moves}):
        ours = [(s, s + delta) for s in range(parts)]
        skip = [sum(v[1] for p, v in plan.items() if p[:2] == k) for k in ours]
        first = table(me, [moves[k][0] + n if k in moves else 0 for k, n in zip(ours, skip)])
        count = table(me, [moves[k][1] - n if k in moves else 0 for k, n in zip(ours, skip)])
        slot0 = table(me, [slot_of(*k) + n if k in moves else 0 for k, n in zip(ours, skip)])
        start = base
        target = lax.rem(me + delta, parts)

        @pl.loop(0, count)
        def _(i):
            copy(
                chunk_of(source_ref, first + i),
                chunk_of(recv_ref, slot0 + i),
                start + i,
                recv_sem.at[slot0 + i],
                target,
            ).start()

        base = base + count

    by_relay = {(r, d - r): (slot_of(s, d) + a, n) for (s, d, r), (a, n) in plan.items()}
    for shift in sorted({k[1] for k in by_relay}):
        mine = [by_relay.get((r, shift), (0, 0)) for r in range(parts)]
        slot0 = table(me, [v[0] for v in mine])
        count = table(me, [v[1] for v in mine])
        start = base
        target = lax.rem(me + shift + parts, parts)

        @pl.loop(0, count)
        def _(i):
            forward = copy(
                held_at(i),
                chunk_of(recv_ref, slot0 + i),
                start + i,
                recv_sem.at[slot0 + i],
                target,
            )
            copy(
                chunk_of(source_ref, jnp.int32(0)), held_at(i), 0, held_sem.at[i], target
            ).wait_recv()
            forward.start()

        base = base + count

    other = lax.rem(me + 1, parts)

    @pl.loop(0, base)
    def _(i):
        copy(
            chunk_of(source_ref, jnp.int32(0)), chunk_of(recv_ref, jnp.int32(0)), i, recv_sem.at[0], other
        ).wait_send()

    got = table(me, received(total, parts)) * SPLIT

    @pl.loop(0, got)
    def _(i):
        copy(
            chunk_of(source_ref, jnp.int32(0)), chunk_of(recv_ref, i), 0, recv_sem.at[i], other
        ).wait_recv()


def received(total, parts):
    moves = flows(total, parts)
    return [sum(n for (s, d), (_, n) in moves.items() if d == r) for r in range(parts)]


def exchange(source, total, parts):
    moves = units(total, parts)
    slots = max(max(received(total, parts)), 2)
    slots += slots % 2
    plan = relays(total, parts)
    sends = max(
        sum(n for (s, d), (_, n) in moves.items() if s == p)
        + sum(n for (_, _, r), (_, n) in plan.items() if r == p)
        for p in range(parts)
    )
    hold = max([n for _, n in plan.values()], default=1)
    return pl.pallas_call(
        functools.partial(exchange_kernel, total, parts),
        out_shape=jax.ShapeDtypeStruct((slots * CHUNK, source.shape[1]), source.dtype),
        in_specs=[pl.BlockSpec(memory_space=pltpu.HBM)],
        out_specs=pl.BlockSpec(memory_space=pltpu.HBM),
        scratch_shapes=[
            pltpu.VMEM((hold * CHUNK, source.shape[1] // SPLIT), source.dtype),
            pltpu.SemaphoreType.DMA((max(sends, 1),)),
            pltpu.SemaphoreType.DMA((slots * SPLIT,)),
            pltpu.SemaphoreType.DMA((hold,)),
        ],
        compiler_params=pltpu.CompilerParams(collective_id=0, has_side_effects=True),
        name="halo",
    )(source)


def split(x):
    high = x.astype(jnp.bfloat16)
    low = (x - high.astype(jnp.float32)).astype(jnp.bfloat16)
    return high, low


def pool_columns(x, levels):
    rows, width = x.shape
    slab = 128 << levels
    i = lax.broadcasted_iota(jnp.int32, (slab, 128), 0)
    o = lax.broadcasted_iota(jnp.int32, (slab, 128), 1)
    pairing = jnp.where(i >> levels == o, 0.5**levels, 0.0).astype(jnp.bfloat16)
    pieces = width // slab
    stacked = jnp.concatenate([x[:, k * slab : (k + 1) * slab] for k in range(pieces)], axis=0)
    high, low = split(stacked)
    out = jnp.dot(high, pairing, preferred_element_type=jnp.float32)
    out = out + jnp.dot(low, pairing, preferred_element_type=jnp.float32)
    return jnp.concatenate([out[k * rows : (k + 1) * rows] for k in range(pieces)], axis=1)


def pyramid_kernel(
    total, parts, low_ref, weight_ref, own_ref, recv_ref, merc_ref, one_ref, two_ref, three_ref, wide
):
    block = own_ref.shape[0]
    slots = recv_ref.shape[0]
    depth = block + slots
    me = lax.axis_index("rows")
    got = table(me, received(total, parts)) * CHUNK

    @pl.when(pl.program_id(0) == 0)
    def _():
        begin = table(me, [w[0] for w in windows(total, parts)])
        low = low_ref[pl.ds(me, 1), :]
        weight = weight_ref[pl.ds(me, 1), :]

        def place(g):
            return jnp.where(g >= me * block, g - me * block, block + g - begin)

        k = lax.broadcasted_iota(jnp.int32, (depth, block), 0)
        band = jnp.where(k == place(low), weight, 0.0)
        band = band + jnp.where(k == place(low + 1), 1.0 - weight, 0.0)
        pools = []
        for level in range(4):
            o = lax.broadcasted_iota(jnp.int32, (block >> level, block), 0)
            i = lax.broadcasted_iota(jnp.int32, (block >> level, block), 1)
            pools.append(jnp.where(i >> level == o, 0.5**level, 0.0).astype(jnp.float32))
        rows = lax.dot_general(
            jnp.concatenate(pools, axis=0),
            band,
            (((1,), (1,)), ((), ())),
            precision=lax.Precision.HIGHEST,
            preferred_element_type=jnp.float32,
        )
        high, low_part = split(rows)
        wide[...] = jnp.concatenate([high, high, low_part], axis=1)

    row = lax.broadcasted_iota(jnp.int32, recv_ref.shape, 0)
    x = jnp.concatenate([own_ref[...], jnp.where(row < got, recv_ref[...], 0.0)], axis=0)
    high, low_part = split(x)
    stacked = jnp.concatenate([high, low_part, high], axis=0)
    y = jnp.dot(wide[...], stacked, preferred_element_type=jnp.float32)
    merc_ref[...] = y[:block]
    at = block
    for level, ref in ((1, one_ref), (2, two_ref)):
        n = block >> level
        ref[...] = pool_columns(y[at : at + n], level)
        at += n
    three = pool_columns(y[at:], 3)
    each = three_ref.shape[1]
    for i in range(three_ref.shape[0]):
        three_ref[i] = three[i * each : (i + 1) * each]


def pyramid(low_row, weight_low, source, recv, total, parts, owners):
    block, width = source.shape
    step = math.gcd(width, STEP)
    slots = recv.shape[0]
    wide_rows = block + block // 2 + block // 4 + block // 8
    each = (block >> 3) // owners
    return pl.pallas_call(
        functools.partial(pyramid_kernel, total, parts),
        grid=(width // step,),
        out_shape=[jax.ShapeDtypeStruct((block >> k, width >> k), jnp.float32) for k in range(3)]
        + [jax.ShapeDtypeStruct((owners, each, width >> 3), jnp.float32)],
        in_specs=[
            pl.BlockSpec((parts, block), lambda j: (0, 0)),
            pl.BlockSpec((parts, block), lambda j: (0, 0)),
            pl.BlockSpec((block, step), lambda j: (0, j)),
            pl.BlockSpec((slots, step), lambda j: (0, j)),
        ],
        out_specs=[pl.BlockSpec((block >> k, step >> k), lambda j: (0, j)) for k in range(3)]
        + [pl.BlockSpec((owners, each, step >> 3), lambda j: (0, 0, j))],
        scratch_shapes=[pltpu.VMEM((wide_rows, 3 * (block + slots)), jnp.bfloat16)],
        name="pyramid",
    )(low_row.reshape(parts, block), weight_low.reshape(parts, block), source, recv)


def share_kernel(owners, three_ref, landed, send_sem, recv_sem, own_sem):
    me = lax.axis_index("cols")
    barrier = pltpu.get_barrier_semaphore()
    for i in range(1, owners):
        pl.semaphore_signal(
            barrier, inc=1, device_id={"cols": lax.rem(me + i, owners)}, device_id_type=MESH
        )
    own = pltpu.make_async_copy(three_ref.at[me], landed.at[0], own_sem)
    own.start()
    pl.semaphore_wait(barrier, owners - 1)
    copies = []
    for i in range(1, owners):
        target = lax.rem(me + i, owners)
        copies.append(
            pltpu.make_async_remote_copy(
                src_ref=three_ref.at[target],
                dst_ref=landed.at[owners - i],
                send_sem=send_sem.at[i],
                recv_sem=recv_sem.at[owners - i],
                device_id={"cols": target},
                device_id_type=MESH,
            )
        )
    for c in copies:
        c.start()
    own.wait()
    for c in copies:
        c.wait()


def finish_kernel(landed, rows_ref, pooled_ref):
    owners, each, width = landed.shape
    me = lax.axis_index("cols")
    pairs = each // 2
    slab = 256
    i = lax.broadcasted_iota(jnp.int32, (slab, 128), 0)
    o = lax.broadcasted_iota(jnp.int32, (slab, 128), 1)
    pairing = jnp.where(i >> 1 == o, 0.25, 0.0).astype(jnp.bfloat16)
    pieces = [landed[lax.rem(c - me + owners, owners)] for c in range(owners)]
    x = jnp.concatenate(pieces, axis=1)
    rows_ref[...] = x
    sums = jnp.concatenate(
        [x[2 * p : 2 * p + 1] + x[2 * p + 1 : 2 * p + 2] for p in range(pairs)], axis=0
    )
    count = owners * width // slab
    flat = jnp.concatenate([sums[:, k * slab : (k + 1) * slab] for k in range(count)], axis=0)
    high, low_part = split(flat)
    out = jnp.dot(high, pairing, preferred_element_type=jnp.float32)
    out = out + jnp.dot(low_part, pairing, preferred_element_type=jnp.float32)
    pooled_ref[...] = jnp.concatenate(
        [out[k * pairs : (k + 1) * pairs] for k in range(count)], axis=1
    )


def share(three):
    owners, each, width = three.shape
    landed = pl.pallas_call(
        functools.partial(share_kernel, owners),
        out_shape=jax.ShapeDtypeStruct(three.shape, jnp.float32),
        in_specs=[pl.BlockSpec(memory_space=pltpu.HBM)],
        out_specs=pl.BlockSpec(memory_space=pltpu.HBM),
        scratch_shapes=[
            pltpu.SemaphoreType.DMA((owners,)),
            pltpu.SemaphoreType.DMA((owners,)),
            pltpu.SemaphoreType.DMA,
        ],
        compiler_params=pltpu.CompilerParams(collective_id=1, has_side_effects=True),
        name="share",
    )(three)
    return pl.pallas_call(
        finish_kernel,
        out_shape=[
            jax.ShapeDtypeStruct((each, owners * width), jnp.float32),
            jax.ShapeDtypeStruct((each // 2, owners * width // 2), jnp.float32),
        ],
        in_specs=[pl.BlockSpec(memory_space=pltpu.VMEM)],
        out_specs=[pl.BlockSpec(memory_space=pltpu.VMEM)] * 2,
        name="finish",
    )(landed)


def body(parts, owners, source, low_row, weight_low):
    total = low_row.shape[0]
    recv = exchange(source, total, parts)
    mercator, level1, level2, three = pyramid(
        low_row, weight_low, source, recv, total, parts, owners
    )
    level3, level4 = share(three)
    return mercator, level1, level2, level3, level4


def solution(mesh):
    return jax.shard_map(
        functools.partial(body, mesh.shape["rows"], mesh.shape["cols"]),
        mesh=mesh,
        in_specs=(P("rows", "cols"), P(), P()),
        out_specs=(
            P("rows", "cols"),
            P("rows", "cols"),
            P("rows", "cols"),
            P(("rows", "cols"), None),
            P(("rows", "cols"), None),
        ),
        check_vma=False,
    )
```

profile of v0, /device:TPU:0, one launch (start us, length us, event | category | flops | bytes accessed | tf_op | source)
XLA Modules:
  0.0 87.7 jit_solution(14758116493581582067)
XLA Ops:
  0.6 72.0 %halo.1.recv_ref = f32[144,8192]{1,0:T(8,128)} custom-call(f32[128,8192]{1,0:T(8,128)} %own_ref.1), custom_call_target="tpu_custom_call" | custom-call | tf_op jit(solution)/shard_map/halo/pallas_call | solution.py:227
  72.6 9.3 %pyramid.1 = (f32[128,8192]{1,0:T(8,128)}, f32[64,4096]{1,0:T(8,128)}, f32[32,2048]{1,0:T(8,128)}, f32[4,4,1024]{2,1,0:T(4,128)}) custom-call(s32[8,128]{1,0:T(8,128)} %bitcast.2, f32[8,128]{1,0:T(8,128)} %bitcast.3, f32[128,8192]{1,0:T(8,128)} %own_ref.1, f32[144,8192]{1,0:T(8,128)} %halo.1.recv_ref), custom_call_target="tpu_custom_call" | custom-call | tf_op jit(solution)/shard_map/pyramid/pallas_call | solution.py:322
  81.9 4.2 %share.1.landed = f32[4,4,1024]{2,1,0:T(4,128)} custom-call(f32[4,4,1024]{2,1,0:T(4,128)} %get-tuple-element.14.three_ref), custom_call_target="tpu_custom_call" | custom-call | tf_op jit(solution)/shard_map/share/pallas_call | solution.py:396
  86.1 1.6 %finish.1 = (f32[4,4096]{1,0:T(4,128)}, f32[2,2048]{1,0:T(2,128)}) custom-call(f32[4,4,1024]{2,1,0:T(4,128)} %share.1.landed), custom_call_target="tpu_custom_call" | custom-call | tf_op jit(solution)/shard_map/finish/pallas_call | solution.py:409
where the time goes:
time: 88 us; the launch traced here: 87.7 us
  Pallas kernels  87.1 us (99%)
    pallas_call x1, Pallas kernels, exchange(): pl.pallas_call(functools.partial(exchange_kernel, total, parts), out_shap...  72 us
    pallas_call x1, Pallas kernels, pyramid(): pl.pallas_call(functools.partial(pyramid_kernel, total, parts), grid=(wid...  9.32 us
    pallas_call x1, Pallas kernels, share(): pl.pallas_call(functools.partial(share_kernel, owners), out_shape=jax.Sha...  4.17 us

commit v1 on v0

v1 whole, which is shorter than its diff:
```python
import functools
import math

import jax
import jax.numpy as jnp
import numpy as np
from jax import lax
from jax.experimental import pallas as pl
from jax.experimental.pallas import tpu as pltpu
from jax.sharding import PartitionSpec as P

LANES = 128
SUB = 8
WIDE = SUB * LANES
JITTER = 2
MESH = pl.DeviceIdType.MESH


def table(index, values):
    out = jnp.int32(values[0])
    for i in range(1, len(values)):
        if values[i] != values[i - 1]:
            out = jnp.where(index >= i, jnp.int32(values[i]), out)
    return out


@functools.lru_cache(maxsize=None)
def windows(total):
    top = 68.0 * math.pi / 180.0
    edge = math.log(math.tan(math.pi / 4 + top / 2))
    m = np.arange(total, dtype=np.float64)
    y = edge * (1.0 - (2.0 * m + 1.0) / (2.0 * total))
    lat = 2.0 * np.arctan(np.exp(y)) - math.pi / 2
    pos = (top - lat) / top * total - 0.5
    slack = 0.01 * total / 1024
    first = np.clip(np.clip(np.floor(pos - slack), 0, total - 2) - JITTER, 0, total - 2)
    last = np.clip(np.clip(np.floor(pos + slack), 0, total - 2) + JITTER, 0, total - 2) + 1
    return first.astype(int), last.astype(int)


@functools.lru_cache(maxsize=None)
def flows(total, parts):
    first, last = windows(total)
    block = total // parts
    found = {}
    for d in range(parts):
        mine = np.arange(d * block, (d + 1) * block)
        for s in range(parts):
            low, high = s * block, (s + 1) * block
            ms = mine[(last[mine] >= low) & (first[mine] < high)]
            if s == d or not len(ms):
                continue
            a, b = max(low, int(first[ms].min())), min(high - 1, int(last[ms].max()))
            m0, n = int(ms.min()), int(ms.max() - ms.min()) + 1
            found[s, d] = (False, a, b - a + 1) if b - a + 1 <= n else (True, m0, n)
    return found


def offsets(total, parts):
    send, recv, sent, got = {}, {}, [0] * parts, [0] * parts
    for (s, d), (_, _, n) in sorted(flows(total, parts).items()):
        send[s, d], recv[s, d] = sent[s], got[d]
        sent[s] += n
        got[d] += n
    return send, recv, sent, got


@functools.lru_cache(maxsize=None)
def relays(total, parts):
    moves = {k: n for k, (_, _, n) in flows(total, parts).items()}
    pairs = parts // 2
    if parts % 2 or min((d - s for s, d in moves), default=1) < 1 or max((d - s for s, d in moves), default=0) > 2:
        return {}
    plan, taken = {}, set()
    load = [moves.get((2 * z, 2 * z + 1), 0) for z in range(pairs)]
    across = 0.0
    for z in range(pairs - 1):
        across += load[z] - sum(load) / pairs
        n = int(round(abs(across)))
        at = z if across > 0 else z + 1
        key, relay = (2 * at, 2 * at + 1), 2 * at + (3 if across > 0 else -1)
        if n and n < moves.get(key, 0) and relay not in taken:
            plan.setdefault(key, {})[relay] = n
            taken.add(relay)
    back = [moves.get((2 * z + 1, 2 * z + 2), 0) for z in range(pairs - 1)]
    goal = sum(back) / pairs
    over = 0
    for z in range(pairs - 1):
        want = int(round(goal * (0.9 if z == 0 else 1.0))) - over
        n = max(0, min(want, back[z]))
        if n and 2 * z not in taken:
            plan.setdefault((2 * z + 1, 2 * z + 2), {})[2 * z] = n
            taken.add(2 * z)
            over = back[z] - n
        else:
            over = back[z]
    return plan


@functools.lru_cache(maxsize=None)
def legs(total, parts):
    send, recv, _, _ = offsets(total, parts)
    whole, out = {}, {}
    for (s, d), (_, _, n) in sorted(flows(total, parts).items()):
        at = 0
        for relay, rows in sorted(relays(total, parts).get((s, d), {}).items()):
            whole[relay - s, False, True, s] = (send[s, d] + at, 0, rows)
            whole[d - relay, True, False, relay] = (0, recv[s, d] + at, rows)
            at += rows
        if n > at:
            whole[d - s, False, False, s] = (send[s, d] + at, recv[s, d] + at, n - at)
    for (hop, relayed, relay, s), (at, to, n) in whole.items():
        done = 0
        for bit in reversed(range(n.bit_length())):
            if n >> bit & 1:
                out.setdefault((hop, relayed, relay, 1 << bit), {})[s] = (at + done, to + done)
                done += 1 << bit
    return sorted(out.items(), key=lambda item: item[0][:3] + (-item[0][3],))


def up(n, k):
    return -(-n // k) * k


def split(x):
    high = x.astype(jnp.bfloat16)
    low = (x - high.astype(jnp.float32)).astype(jnp.bfloat16)
    return high, low


def iota(shape, axis):
    return lax.broadcasted_iota(jnp.int32, shape, axis)


def pool_columns(x, levels):
    rows, width = x.shape
    slab = LANES << levels
    pairing = jnp.where(
        iota((slab, LANES), 0) >> levels == iota((slab, LANES), 1), 0.5**levels, 0.0
    ).astype(jnp.bfloat16)
    pieces = width // slab
    stacked = jnp.concatenate([x[:, k * slab : (k + 1) * slab] for k in range(pieces)], axis=0)
    high, low = split(stacked)
    out = jnp.dot(high, pairing, preferred_element_type=jnp.float32)
    out = out + jnp.dot(low, pairing, preferred_element_type=jnp.float32)
    return jnp.concatenate([out[k * rows : (k + 1) * rows] for k in range(pieces)], axis=1)


def exact_dot(a, b):
    return lax.dot_general(
        a,
        b,
        (((1,), (1,)), ((), ())),
        precision=lax.Precision.HIGHEST,
        preferred_element_type=jnp.float32,
    )


def flow_tables(total, parts, me, delta, kind, sending):
    send, recv, _, _ = offsets(total, parts)
    rows, place, first = [], [], []
    for i in range(parts):
        key = (i, i + delta) if sending else (i - delta, i)
        what = flows(total, parts).get(key)
        good = what is not None and what[0] == kind
        rows.append(what[2] if good else 0)
        place.append((send if sending else recv)[key] if good else 0)
        first.append(what[1] if good else 0)
    return table(me, rows), table(me, place), table(me, first)


def hops(total, parts, kind):
    return sorted({d - s for (s, d), what in flows(total, parts).items() if what[0] == kind})


def send_weights(total, parts, me, block, rows, low_ref, weight_ref):
    k, c = iota((rows, block), 0), iota((rows, block), 1)
    out = jnp.zeros((rows, block), jnp.float32)
    for delta in hops(total, parts, False):
        n, at, first = flow_tables(total, parts, me, delta, False, True)
        here = (k >= at) & (k < at + n)
        out = out + jnp.where(here & (c == k - at + first - me * block), 1.0, 0.0)
    for delta in hops(total, parts, True):
        n, at, first = flow_tables(total, parts, me, delta, True, True)
        owner = jnp.clip(me + delta, 0, parts - 1)
        low = low_ref[pl.ds(owner, 1), :] - me * block
        weight = weight_ref[pl.ds(owner, 1), :]
        row = iota((block, block), 0)
        band = jnp.where(row == low, weight, 0.0) + jnp.where(row == low + 1, 1.0 - weight, 0.0)
        pick = (k >= at) & (k < at + n) & (c == k - at + first - owner * block)
        out = out + exact_dot(jnp.where(pick, 1.0, 0.0), band)
    high, low_part = split(out)
    return jnp.concatenate([high, high, low_part], axis=1)


def own_weights(total, parts, me, block, slots, low_ref, weight_ref):
    low = low_ref[pl.ds(me, 1), :]
    weight = weight_ref[pl.ds(me, 1), :]

    def rows_of(g, valid):
        out = jnp.where(valid & (g == low), weight, 0.0)
        return out + jnp.where(valid & (g == low + 1), 1.0 - weight, 0.0)

    own = iota((block, block), 0) + me * block
    k, m = iota((slots, block), 0), iota((slots, block), 1)
    far = jnp.zeros((slots, block), jnp.float32)
    for delta in hops(total, parts, False):
        n, at, first = flow_tables(total, parts, me, delta, False, False)
        far = far + rows_of(k - at + first, (k >= at) & (k < at + n))
    for delta in hops(total, parts, True):
        n, at, first = flow_tables(total, parts, me, delta, True, False)
        here = (k >= at) & (k < at + n) & (m == k - at + first - me * block)
        far = far + jnp.where(here, 1.0, 0.0)
    band = jnp.concatenate([rows_of(own, own >= 0), far], axis=0)
    pools = []
    for level in range(4):
        o, i = iota((block >> level, block), 0), iota((block >> level, block), 1)
        pools.append(jnp.where(i >> level == o, 0.5**level, 0.0).astype(jnp.float32))
    high, low_part = split(exact_dot(jnp.concatenate(pools, axis=0), band))
    return jnp.concatenate([high, high, low_part], axis=1)


def fused_kernel(
    total, parts, owners,
    low_ref, weight_ref, source_ref,
    merc_ref, one_ref, two_ref, rows_ref, pooled_ref,
    own, sent, recv, held, three, landed, out_w, in_w,
    own_sem, send_sem, recv_sem, share_send, share_recv,
):
    block, width = source_ref.shape
    chunks = width // WIDE
    me, col = lax.axis_index("rows"), lax.axis_index("cols")
    groups = legs(total, parts)
    got = table(me, offsets(total, parts)[3])
    slots = recv.shape[1]
    send_rows = sent.shape[1]

    def columns(j, size):
        return pl.ds(pl.multiple_of(j * size, size), size)

    def load(j):
        at = columns(j, WIDE)
        return pltpu.make_async_copy(source_ref.at[:, at], own.at[:, at], own_sem.at[j])

    @pl.loop(0, chunks)
    def _(j):
        load(j).start()

    barrier = pltpu.get_barrier_semaphore()
    greet = {}
    for (hop, _, _, _), by in groups:
        for s in by:
            greet.setdefault(hop, set()).add(s)
            greet.setdefault(-hop, set()).add(s + hop)
    for hop, who in sorted(greet.items()):
        @pl.when(table(me, [int(i in who) for i in range(parts)]) > 0)
        def _():
            pl.semaphore_signal(barrier, inc=1, device_id={"rows": me + hop}, device_id_type=MESH)

    for i in range(1, owners):
        pl.semaphore_signal(
            barrier, inc=1, device_id={"cols": lax.rem(col + i, owners)}, device_id_type=MESH
        )
    waits = [sum(i in who for who in greet.values()) + owners - 1 for i in range(parts)]

    def copy(g, j, src, dst, target):
        return pltpu.make_async_remote_copy(
            src_ref=src,
            dst_ref=dst,
            send_sem=send_sem.at[g, j],
            recv_sem=recv_sem.at[g, j],
            device_id={"rows": target},
            device_id_type=MESH,
        )

    def leaving(g, j, act):
        (hop, relayed, to_relay, n), by = groups[g]
        at, to = (table(me, [by.get(i, (0, 0))[f] for i in range(parts)]) for f in range(2))
        src, dst = (held if relayed else sent), (held if to_relay else recv)

        @pl.when(table(me, [int(i in by) for i in range(parts)]) > 0)
        def _():
            act(copy(g, j, src.at[j, pl.ds(at, n)], dst.at[j, pl.ds(to, n)], me + hop))

    def arriving(g, j):
        (hop, _, to_relay, n), by = groups[g]
        to = table(me, [by.get(i - hop, (0, 0))[1] for i in range(parts)])
        dst = held if to_relay else recv

        @pl.when(table(me, [int(i - hop in by) for i in range(parts)]) > 0)
        def _():
            there = dst.at[j, pl.ds(to, n)]
            copy(g, j, there, there, me - hop).wait_recv()

    first_hop = [g for g, ((_, relayed, _, _), _) in enumerate(groups) if not relayed]
    second_hop = [g for g, ((_, relayed, _, _), _) in enumerate(groups) if relayed]
    to_relay = [g for g, ((_, _, relay, _), _) in enumerate(groups) if relay]
    to_owner = [g for g, ((_, _, relay, _), _) in enumerate(groups) if not relay]
    first_hop.sort(key=lambda g: g not in to_relay)

    out_w[...] = send_weights(total, parts, me, block, send_rows, low_ref, weight_ref)
    sent_rows = sent.reshape(chunks, send_rows * SUB, LANES)
    recv_rows = recv.reshape(chunks, slots * SUB, LANES)

    def prepare(j):
        load(j).wait()
        high, low_part = split(own[:, columns(j, WIDE)])
        y = jnp.dot(
            out_w[...],
            jnp.concatenate([high, low_part, high], axis=0),
            preferred_element_type=jnp.float32,
        )
        for b in range(SUB):
            sent_rows[j, pl.ds(b, send_rows, stride=SUB), :] = y[:, b * LANES : (b + 1) * LANES]

    def dispatch(j):
        for g in first_hop:
            leaving(g, j, lambda c: c.start())

    prepare(0)
    pl.semaphore_wait(barrier, table(me, waits))
    dispatch(0)

    @pl.loop(1, chunks)
    def _(j):
        prepare(j)
        dispatch(j)

    in_w[...] = own_weights(total, parts, me, block, slots, low_ref, weight_ref)

    def forward(j):
        for g in to_relay:
            arriving(g, j)
        for g in second_hop:
            leaving(g, j, lambda c: c.start())

    forward(0)

    @pl.loop(0, chunks)
    def _(j):
        @pl.when(j + 1 < chunks)
        def _():
            forward(j + 1)

        for g in to_owner:
            arriving(g, j)
        row = iota((slots, LANES), 0)
        far = [
            jnp.where(row < got, recv_rows[j, pl.ds(b, slots, stride=SUB), :], 0.0)
            for b in range(SUB)
        ]
        x = jnp.concatenate([own[:, columns(j, WIDE)], jnp.concatenate(far, axis=1)], axis=0)
        high, low_part = split(x)
        y = jnp.dot(
            in_w[...],
            jnp.concatenate([high, low_part, high], axis=0),
            preferred_element_type=jnp.float32,
        )
        merc_ref[:, columns(j, WIDE)] = y[:block]
        at = block
        for level, ref in ((1, one_ref), (2, two_ref)):
            n = block >> level
            ref[:, columns(j, WIDE >> level)] = pool_columns(y[at : at + n], level)
            at += n
        pooled = pool_columns(y[at:], 3)
        each = three.shape[1]
        for i in range(owners):
            three[i, :, columns(j, WIDE >> 3)] = pooled[i * each : (i + 1) * each]

    shares = []
    for i in range(1, owners):
        target = lax.rem(col + i, owners)
        shares.append(
            pltpu.make_async_remote_copy(
                src_ref=three.at[target],
                dst_ref=landed.at[owners - i],
                send_sem=share_send.at[i],
                recv_sem=share_recv.at[owners - i],
                device_id={"cols": target},
                device_id_type=MESH,
            )
        )
    for c in shares:
        c.start()

    @pl.loop(0, chunks)
    def _(j):
        for g in range(len(groups)):
            leaving(g, j, lambda c: c.wait_send())

    landed[0] = three[col]
    for c in shares:
        c.wait()
    finish(owners, col, landed, rows_ref, pooled_ref)


def finish(owners, col, landed, rows_ref, pooled_ref):
    _, each, width = landed.shape
    pairs = each // 2
    slab = 2 * LANES
    pairing = jnp.where(
        iota((slab, LANES), 0) >> 1 == iota((slab, LANES), 1), 0.25, 0.0
    ).astype(jnp.bfloat16)
    x = jnp.concatenate([landed[lax.rem(c - col + owners, owners)] for c in range(owners)], axis=1)
    rows_ref[...] = x
    sums = jnp.concatenate(
        [x[2 * p : 2 * p + 1] + x[2 * p + 1 : 2 * p + 2] for p in range(pairs)], axis=0
    )
    count = owners * width // slab
    flat = jnp.concatenate([sums[:, k * slab : (k + 1) * slab] for k in range(count)], axis=0)
    high, low_part = split(flat)
    out = jnp.dot(high, pairing, preferred_element_type=jnp.float32)
    out = out + jnp.dot(low_part, pairing, preferred_element_type=jnp.float32)
    pooled_ref[...] = jnp.concatenate(
        [out[k * pairs : (k + 1) * pairs] for k in range(count)], axis=1
    )


def write_kernel(*refs):
    n = len(refs) // 2
    sems = refs[2 * n]
    copies = [pltpu.make_async_copy(refs[i], refs[n + i], sems.at[i]) for i in range(n)]
    for c in copies:
        c.start()
    for c in copies:
        c.wait()


def body(parts, owners, source, low_row, weight_low):
    total = low_row.shape[0]
    block, width = source.shape
    _, _, sent, got = offsets(total, parts)
    send_rows, slots = up(max(sent), 16), up(max(got), 16)
    hold = max([n for by in relays(total, parts).values() for n in by.values()], default=1)
    groups = max(len(legs(total, parts)), 1)
    chunks = width // WIDE
    each = (block >> 3) // owners
    wide_rows = block + block // 2 + block // 4 + block // 8
    f32 = jnp.float32
    shapes = [(block >> k, width >> k) for k in range(3)]
    shapes += [(each, owners * (width >> 3)), (each // 2, owners * (width >> 4))]
    vmem = pl.BlockSpec(memory_space=pltpu.VMEM)
    hbm = pl.BlockSpec(memory_space=pltpu.HBM)
    outs = pl.pallas_call(
        functools.partial(fused_kernel, total, parts, owners),
        out_shape=[pltpu.VMEM(s, f32) for s in shapes],
        in_specs=[vmem, vmem, hbm],
        out_specs=[vmem] * len(shapes),
        scratch_shapes=[
            pltpu.VMEM((block, width), f32),
            pltpu.VMEM((chunks, send_rows, SUB, LANES), f32),
            pltpu.VMEM((chunks, slots, SUB, LANES), f32),
            pltpu.VMEM((chunks, hold, SUB, LANES), f32),
            pltpu.VMEM((owners, each, width >> 3), f32),
            pltpu.VMEM((owners, each, width >> 3), f32),
            pltpu.VMEM((send_rows, 3 * block), jnp.bfloat16),
            pltpu.VMEM((wide_rows, 3 * (block + slots)), jnp.bfloat16),
            pltpu.SemaphoreType.DMA((chunks,)),
            pltpu.SemaphoreType.DMA((groups, chunks)),
            pltpu.SemaphoreType.DMA((groups, chunks)),
            pltpu.SemaphoreType.DMA((owners,)),
            pltpu.SemaphoreType.DMA((owners,)),
        ],
        compiler_params=pltpu.CompilerParams(
            collective_id=0, has_side_effects=True, vmem_limit_bytes=54 << 20
        ),
        name="reproject",
    )(low_row.reshape(parts, block), weight_low.reshape(parts, block), source)
    return pl.pallas_call(
        write_kernel,
        out_shape=[jax.ShapeDtypeStruct(s, f32) for s in shapes],
        in_specs=[vmem] * len(shapes),
        out_specs=[hbm] * len(shapes),
        scratch_shapes=[pltpu.SemaphoreType.DMA((len(shapes),))],
        compiler_params=pltpu.CompilerParams(vmem_limit_bytes=8 << 20),
        name="write",
    )(*outs)


def solution(mesh):
    return jax.shard_map(
        functools.partial(body, mesh.shape["rows"], mesh.shape["cols"]),
        mesh=mesh,
        in_specs=(P("rows", "cols"), P(), P()),
        out_specs=(
            P("rows", "cols"),
            P("rows", "cols"),
            P("rows", "cols"),
            P(("rows", "cols"), None),
            P(("rows", "cols"), None),
        ),
        check_vma=False,
    )
```

time: 88 us -> 73.8 us (0.84)
  the two profiles are of different devices: /device:TPU:0 before, /device:TPU:19 now
where the time goes in v1:
time: 73.8 us; the launch traced here: 73.6 us
  Pallas kernels  72.9 us (99%)
    pallas_call x1, Pallas kernels, body(): pl.pallas_call(functools.partial(fused_kernel, total, parts, owners), out...  70.5 us
    pallas_call x1, Pallas kernels, body(): pl.pallas_call(write_kernel, out_shape=[jax.ShapeDtypeStruct(s, f32) for...  2.45 us

profile of v1, /device:TPU:19, one launch (start us, length us, event | category | flops | bytes accessed | tf_op | source)
XLA Modules:
  0.0 73.6 jit_solution(16579021187640443202)
XLA Ops:
  0.6 70.5 %reproject.1 = (f32[128,8192]{1,0:T(8,128)S(1)}, f32[64,4096]{1,0:T(8,128)S(1)}, f32[32,2048]{1,0:T(8,128)S(1)}, f32[4,4096]{1,0:T(4,128)S(1)}, f32[2,2048]{1,0:T(2,128)S(1)}) custom-call(s32[8,128]{1,0:T(8,128)} %bitcast.2, f32[8,128]{1,0:T(8,128)} %bitcast.3, f32[128,8192]{1,0:T(8,128)} %source_ref.1), custom_call_target="tpu_custom_call" | custom-call | tf_op jit(solution)/shard_map/reproject/pallas_call | solution.py:444
  71.1 2.5 %write.1 = (f32[128,8192]{1,0:T(8,128)}, f32[64,4096]{1,0:T(8,128)}, f32[32,2048]{1,0:T(8,128)}, f32[4,4096]{1,0:T(4,128)}, f32[2,2048]{1,0:T(2,128)}) custom-call(f32[128,8192]{1,0:T(8,128)S(1)} %get-tuple-element.10.refs_0_, f32[64,4096]{1,0:T(8,128)S(1)} %get-tuple-element.11.refs_1_, f32[32,2048]{1,0:T(8,128)S(1)} %get-tuple-element.12.refs_2_, ...), custom_call_target="tpu_custom_call" | custom-call | tf_op jit(solution)/shard_map/write/pallas_call | solution.py:469

commit v2 on v1

--- a/solution.py
+++ b/solution.py
@@ -100,22 +100,22 @@
 @functools.lru_cache(maxsize=None)
 def legs(total, parts):
     send, recv, _, _ = offsets(total, parts)
-    whole, out = {}, {}
+    found = []
     for (s, d), (_, _, n) in sorted(flows(total, parts).items()):
         at = 0
         for relay, rows in sorted(relays(total, parts).get((s, d), {}).items()):
-            whole[relay - s, False, True, s] = (send[s, d] + at, 0, rows)
-            whole[d - relay, True, False, relay] = (0, recv[s, d] + at, rows)
+            found.append((s, relay, False, True, send[s, d] + at, 0, rows))
+            found.append((relay, d, True, False, 0, recv[s, d] + at, rows))
             at += rows
         if n > at:
-            whole[d - s, False, False, s] = (send[s, d] + at, recv[s, d] + at, n - at)
-    for (hop, relayed, relay, s), (at, to, n) in whole.items():
-        done = 0
-        for bit in reversed(range(n.bit_length())):
-            if n >> bit & 1:
-                out.setdefault((hop, relayed, relay, 1 << bit), {})[s] = (at + done, to + done)
-                done += 1 << bit
-    return sorted(out.items(), key=lambda item: item[0][:3] + (-item[0][3],))
+            found.append((s, d, False, False, send[s, d] + at, recv[s, d] + at, n - at))
+    found.sort(key=lambda leg: not leg[3])
+    left, come, out = [0] * parts, [0] * parts, []
+    for leg in found:
+        out.append(leg + (left[leg[0]], come[leg[1]]))
+        left[leg[0]] += 1
+        come[leg[1]] += 1
+    return out
 
 
 def up(n, k):
@@ -246,57 +246,52 @@
     def _(j):
         load(j).start()
 
+    def by_device(chosen, act, where):
+        for i in range(parts):
+            mine = [leg for leg in chosen if leg[where] == i]
+
+            if mine:
+                @pl.when(me == i)
+                def _():
+                    for leg in mine:
+                        act(leg)
+
     barrier = pltpu.get_barrier_semaphore()
-    greet = {}
-    for (hop, _, _, _), by in groups:
-        for s in by:
-            greet.setdefault(hop, set()).add(s)
-            greet.setdefault(-hop, set()).add(s + hop)
-    for hop, who in sorted(greet.items()):
-        @pl.when(table(me, [int(i in who) for i in range(parts)]) > 0)
+    met = [sorted({a[1 - k] for a in groups for k in (0, 1) if a[k] == i}) for i in range(parts)]
+    for i in range(parts):
+        @pl.when(me == i)
         def _():
-            pl.semaphore_signal(barrier, inc=1, device_id={"rows": me + hop}, device_id_type=MESH)
+            for other in met[i]:
+                pl.semaphore_signal(barrier, inc=1, device_id={"rows": other}, device_id_type=MESH)
 
     for i in range(1, owners):
         pl.semaphore_signal(
             barrier, inc=1, device_id={"cols": lax.rem(col + i, owners)}, device_id_type=MESH
         )
-    waits = [sum(i in who for who in greet.values()) + owners - 1 for i in range(parts)]
-
-    def copy(g, j, src, dst, target):
+    waits = [len(met[i]) + owners - 1 for i in range(parts)]
+
+    def copy(leg, j):
+        _, target, relayed, to_relay, at, to, n, left, come = leg
+        src, dst = (held if relayed else sent), (held if to_relay else recv)
         return pltpu.make_async_remote_copy(
-            src_ref=src,
-            dst_ref=dst,
-            send_sem=send_sem.at[g, j],
-            recv_sem=recv_sem.at[g, j],
+            src_ref=src.at[j, pl.ds(at, n)],
+            dst_ref=dst.at[j, pl.ds(to, n)],
+            send_sem=send_sem.at[left, j],
+            recv_sem=recv_sem.at[come, j],
             device_id={"rows": target},
             device_id_type=MESH,
         )
 
-    def leaving(g, j, act):
-        (hop, relayed, to_relay, n), by = groups[g]
-        at, to = (table(me, [by.get(i, (0, 0))[f] for i in range(parts)]) for f in range(2))
-        src, dst = (held if relayed else sent), (held if to_relay else recv)
-
-        @pl.when(table(me, [int(i in by) for i in range(parts)]) > 0)
-        def _():
-            act(copy(g, j, src.at[j, pl.ds(at, n)], dst.at[j, pl.ds(to, n)], me + hop))
-
-    def arriving(g, j):
-        (hop, _, to_relay, n), by = groups[g]
-        to = table(me, [by.get(i - hop, (0, 0))[1] for i in range(parts)])
-        dst = held if to_relay else recv
-
-        @pl.when(table(me, [int(i - hop in by) for i in range(parts)]) > 0)
-        def _():
-            there = dst.at[j, pl.ds(to, n)]
-            copy(g, j, there, there, me - hop).wait_recv()
-
-    first_hop = [g for g, ((_, relayed, _, _), _) in enumerate(groups) if not relayed]
-    second_hop = [g for g, ((_, relayed, _, _), _) in enumerate(groups) if relayed]
-    to_relay = [g for g, ((_, _, relay, _), _) in enumerate(groups) if relay]
-    to_owner = [g for g, ((_, _, relay, _), _) in enumerate(groups) if not relay]
-    first_hop.sort(key=lambda g: g not in to_relay)
+    def leave(chosen, j):
+        by_device(chosen, lambda leg: copy(leg, j).start(), 0)
+
+    def arrive(chosen, j):
+        by_device(chosen, lambda leg: copy(leg, j).wait_recv(), 1)
+
+    first_hop = [leg for leg in groups if not leg[2]]
+    second_hop = [leg for leg in groups if leg[2]]
+    to_relay = [leg for leg in groups if leg[3]]
+    to_owner = [leg for leg in groups if not leg[3]]
 
     out_w[...] = send_weights(total, parts, me, block, send_rows, low_ref, weight_ref)
     sent_rows = sent.reshape(chunks, send_rows * SUB, LANES)
@@ -313,26 +308,20 @@
         for b in range(SUB):
             sent_rows[j, pl.ds(b, send_rows, stride=SUB), :] = y[:, b * LANES : (b + 1) * LANES]
 
-    def dispatch(j):
-        for g in first_hop:
-            leaving(g, j, lambda c: c.start())
-
     prepare(0)
     pl.semaphore_wait(barrier, table(me, waits))
-    dispatch(0)
+    leave(first_hop, 0)
 
     @pl.loop(1, chunks)
     def _(j):
         prepare(j)
-        dispatch(j)
+        leave(first_hop, j)
 
     in_w[...] = own_weights(total, parts, me, block, slots, low_ref, weight_ref)
 
     def forward(j):
-        for g in to_relay:
-            arriving(g, j)
-        for g in second_hop:
-            leaving(g, j, lambda c: c.start())
+        arrive(to_relay, j)
+        leave(second_hop, j)
 
     forward(0)
 
@@ -342,8 +331,7 @@
         def _():
             forward(j + 1)
 
-        for g in to_owner:
-            arriving(g, j)
+        arrive(to_owner, j)
         row = iota((slots, LANES), 0)
         far = [
             jnp.where(row < got, recv_rows[j, pl.ds(b, slots, stride=SUB), :], 0.0)
@@ -385,8 +373,7 @@
 
     @pl.loop(0, chunks)
     def _(j):
-        for g in range(len(groups)):
-            leaving(g, j, lambda c: c.wait_send())
+        by_device(groups, lambda leg: copy(leg, j).wait_send(), 0)
 
     landed[0] = three[col]
     for c in shares:
@@ -432,7 +419,8 @@
     _, _, sent, got = offsets(total, parts)
     send_rows, slots = up(max(sent), 16), up(max(got), 16)
     hold = max([n for by in relays(total, parts).values() for n in by.values()], default=1)
-    groups = max(len(legs(total, parts)), 1)
+    left = max([leg[7] + 1 for leg in legs(total, parts)], default=1)
+    come = max([leg[8] + 1 for leg in legs(total, parts)], default=1)
     chunks = width // WIDE
     each = (block >> 3) // owners
     wide_rows = block + block // 2 + block // 4 + block // 8
@@ -456,8 +444,8 @@
             pltpu.VMEM((send_rows, 3 * block), jnp.bfloat16),
             pltpu.VMEM((wide_rows, 3 * (block + slots)), jnp.bfloat16),
             pltpu.SemaphoreType.DMA((chunks,)),
-            pltpu.SemaphoreType.DMA((groups, chunks)),
-            pltpu.SemaphoreType.DMA((groups, chunks)),
+            pltpu.SemaphoreType.DMA((left, chunks)),
+            pltpu.SemaphoreType.DMA((come, chunks)),
             pltpu.SemaphoreType.DMA((owners,)),
             pltpu.SemaphoreType.DMA((owners,)),
         ],

time: 73.8 us -> 69.8 us (0.946)
  Pallas kernels: 72.9 us -> 68.9 us
    pallas_call x1, Pallas kernels: 70.5 us -> 66.5 us  [body(): pl.pallas_call(functools.partial(fused_kernel, total, parts, owners), out...]
where the time goes in v2:
time: 69.8 us; the launch traced here: 69.6 us
  Pallas kernels  68.9 us (99%)
    pallas_call x1, Pallas kernels, body(): pl.pallas_call(functools.partial(fused_kernel, total, parts, owners), out...  66.5 us
    pallas_call x1, Pallas kernels, body(): pl.pallas_call(write_kernel, out_shape=[jax.ShapeDtypeStruct(s, f32) for...  2.45 us

profile of v2, /device:TPU:19, one launch (start us, length us, event | category | flops | bytes accessed | tf_op | source)
XLA Modules:
  0.0 69.6 jit_solution(17267708396565034586)
XLA Ops:
  0.6 66.5 %reproject.1 = (f32[128,8192]{1,0:T(8,128)S(1)}, f32[64,4096]{1,0:T(8,128)S(1)}, f32[32,2048]{1,0:T(8,128)S(1)}, f32[4,4096]{1,0:T(4,128)S(1)}, f32[2,2048]{1,0:T(2,128)S(1)}) custom-call(s32[8,128]{1,0:T(8,128)} %bitcast.2, f32[8,128]{1,0:T(8,128)} %bitcast.3, f32[128,8192]{1,0:T(8,128)} %source_ref.1), custom_call_target="tpu_custom_call" | custom-call | tf_op jit(solution)/shard_map/reproject/pallas_call | solution.py:432
  67.1 2.5 %write.1 = (f32[128,8192]{1,0:T(8,128)}, f32[64,4096]{1,0:T(8,128)}, f32[32,2048]{1,0:T(8,128)}, f32[4,4096]{1,0:T(4,128)}, f32[2,2048]{1,0:T(2,128)}) custom-call(f32[128,8192]{1,0:T(8,128)S(1)} %get-tuple-element.10.refs_0_, f32[64,4096]{1,0:T(8,128)S(1)} %get-tuple-element.11.refs_1_, f32[32,2048]{1,0:T(8,128)S(1)} %get-tuple-element.12.refs_2_, ...), custom_call_target="tpu_custom_call" | custom-call | tf_op jit(solution)/shard_map/write/pallas_call | solution.py:457

commit v3 on v2

--- a/solution.py
+++ b/solution.py
@@ -13,6 +13,7 @@
 SUB = 8
 WIDE = SUB * LANES
 JITTER = 2
+HINTED = 2
 MESH = pl.DeviceIdType.MESH
 
 
@@ -97,6 +98,10 @@
     return plan
 
 
+def halves(n):
+    return [(0, n // 2), (n // 2, n - n // 2)] if n > 1 else [(0, n)]
+
+
 @functools.lru_cache(maxsize=None)
 def legs(total, parts):
     send, recv, _, _ = offsets(total, parts)
@@ -104,18 +109,13 @@
     for (s, d), (_, _, n) in sorted(flows(total, parts).items()):
         at = 0
         for relay, rows in sorted(relays(total, parts).get((s, d), {}).items()):
-            found.append((s, relay, False, True, send[s, d] + at, 0, rows))
-            found.append((relay, d, True, False, 0, recv[s, d] + at, rows))
+            for half, (low, n_part) in enumerate(halves(rows)):
+                found.append((s, relay, False, True, send[s, d] + at + low, low, n_part, half))
+                found.append((relay, d, True, False, low, recv[s, d] + at + low, n_part, half))
             at += rows
         if n > at:
-            found.append((s, d, False, False, send[s, d] + at, recv[s, d] + at, n - at))
-    found.sort(key=lambda leg: not leg[3])
-    left, come, out = [0] * parts, [0] * parts, []
-    for leg in found:
-        out.append(leg + (left[leg[0]], come[leg[1]]))
-        left[leg[0]] += 1
-        come[leg[1]] += 1
-    return out
+            found.append((s, d, False, False, send[s, d] + at, recv[s, d] + at, n - at, 0))
+    return sorted(found, key=lambda leg: not leg[3])
 
 
 def up(n, k):
@@ -193,6 +193,28 @@
     return jnp.concatenate([high, high, low_part], axis=1)
 
 
+def pool_rows(block, level):
+    o, i = iota((block >> level, block), 0), iota((block >> level, block), 1)
+    return jnp.where(i >> level == o, 0.5**level, 0.0).astype(jnp.float32)
+
+
+def all_hops(total, parts):
+    return sorted({d - s for s, d in flows(total, parts)})
+
+
+def coarse_weights(total, parts, me, block, low_ref, weight_ref):
+    out = []
+    row = iota((block, block), 0)
+    for delta in [0] + all_hops(total, parts):
+        owner = jnp.clip(me + delta, 0, parts - 1)
+        low = low_ref[pl.ds(owner, 1), :] - me * block
+        weight = weight_ref[pl.ds(owner, 1), :]
+        band = jnp.where(row == low, weight, 0.0) + jnp.where(row == low + 1, 1.0 - weight, 0.0)
+        out.append(exact_dot(pool_rows(block, 3), band))
+    high, low_part = split(jnp.concatenate(out, axis=0))
+    return jnp.concatenate([high, high, low_part], axis=1)
+
+
 def own_weights(total, parts, me, block, slots, low_ref, weight_ref):
     low = low_ref[pl.ds(me, 1), :]
     weight = weight_ref[pl.ds(me, 1), :]
@@ -212,39 +234,70 @@
         here = (k >= at) & (k < at + n) & (m == k - at + first - me * block)
         far = far + jnp.where(here, 1.0, 0.0)
     band = jnp.concatenate([rows_of(own, own >= 0), far], axis=0)
-    pools = []
-    for level in range(4):
-        o, i = iota((block >> level, block), 0), iota((block >> level, block), 1)
-        pools.append(jnp.where(i >> level == o, 0.5**level, 0.0).astype(jnp.float32))
+    pools = [pool_rows(block, level) for level in range(4)]
     high, low_part = split(exact_dot(jnp.concatenate(pools, axis=0), band))
     return jnp.concatenate([high, high, low_part], axis=1)
 
 
+def columns(j, size):
+    return pl.ds(pl.multiple_of(j * size, size), size)
+
+
+def triple(x):
+    high, low_part = split(x)
+    return jnp.concatenate([high, low_part, high], axis=0)
+
+
+def dot(a, b):
+    return jnp.dot(a, b, preferred_element_type=jnp.float32)
+
+
+def chunk_rows(total, parts, j, own, recv, in_w, levels):
+    block, (chunks, slots) = own.shape[0], recv.shape[:2]
+    got = table(lax.axis_index("rows"), offsets(total, parts)[3])
+    rows = recv.reshape(chunks, slots * SUB, LANES)
+    row = iota((slots, LANES), 0)
+    far = [
+        jnp.where(row < got, rows[j, pl.ds(b, slots, stride=SUB), :], 0.0) for b in range(SUB)
+    ]
+    x = jnp.concatenate([own[:, columns(j, WIDE)], jnp.concatenate(far, axis=1)], axis=0)
+    y = dot(in_w[: 2 * block - (block >> levels), :], triple(x))
+    out, at = [], 0
+    for level in range(levels + 1):
+        out.append(y[at : at + (block >> level)])
+        at += block >> level
+    return out
+
+
 def fused_kernel(
     total, parts, owners,
-    low_ref, weight_ref, source_ref,
-    merc_ref, one_ref, two_ref, rows_ref, pooled_ref,
-    own, sent, recv, held, three, landed, out_w, in_w,
-    own_sem, send_sem, recv_sem, share_send, share_recv,
+    low_hbm, weight_hbm, source_ref,
+    merc_ref, one_ref, two_ref, rows_ref, pooled_ref, own, recv, in_w,
+    low_ref, weight_ref, sent, held, three, landed, out_w, coarse_w, early, hint,
+    small_sem, own_sem, send_sem, recv_sem, held_sem, early_send, early_recv, share_sem,
 ):
     block, width = source_ref.shape
     chunks = width // WIDE
     me, col = lax.axis_index("rows"), lax.axis_index("cols")
     groups = legs(total, parts)
-    got = table(me, offsets(total, parts)[3])
+    _, _, rows_out, rows_in = offsets(total, parts)
     slots = recv.shape[1]
     send_rows = sent.shape[1]
-
-    def columns(j, size):
-        return pl.ds(pl.multiple_of(j * size, size), size)
-
-    def load(j):
-        at = columns(j, WIDE)
-        return pltpu.make_async_copy(source_ref.at[:, at], own.at[:, at], own_sem.at[j])
-
-    @pl.loop(0, chunks)
-    def _(j):
-        load(j).start()
+    each = three.shape[1]
+    hop_list = all_hops(total, parts)
+
+    loads = [
+        pltpu.make_async_copy(source_ref.at[:, at], own.at[:, at], own_sem.at[i])
+        for i, at in enumerate((pl.ds(0, WIDE), pl.ds(WIDE, width - WIDE)))
+    ]
+
+    small = [
+        pltpu.make_async_copy(low_hbm, low_ref, small_sem.at[0]),
+        pltpu.make_async_copy(weight_hbm, weight_ref, small_sem.at[1]),
+    ]
+    for c in small:
+        c.start()
+    loads[0].start()
 
     def by_device(chosen, act, where):
         for i in range(parts):
@@ -257,7 +310,8 @@
                         act(leg)
 
     barrier = pltpu.get_barrier_semaphore()
-    met = [sorted({a[1 - k] for a in groups for k in (0, 1) if a[k] == i}) for i in range(parts)]
+    ties = [leg[:2] for leg in groups] + list(flows(total, parts))
+    met = [sorted({a[1 - k] for a in ties for k in (0, 1) if a[k] == i}) for i in range(parts)]
     for i in range(parts):
         @pl.when(me == i)
         def _():
@@ -270,14 +324,16 @@
         )
     waits = [len(met[i]) + owners - 1 for i in range(parts)]
 
+    loads[1].start()
+
     def copy(leg, j):
-        _, target, relayed, to_relay, at, to, n, left, come = leg
+        _, target, relayed, to_relay, at, to, n, half = leg
         src, dst = (held if relayed else sent), (held if to_relay else recv)
         return pltpu.make_async_remote_copy(
             src_ref=src.at[j, pl.ds(at, n)],
             dst_ref=dst.at[j, pl.ds(to, n)],
-            send_sem=send_sem.at[left, j],
-            recv_sem=recv_sem.at[come, j],
+            send_sem=send_sem.at[int(relayed)],
+            recv_sem=held_sem.at[half, j] if to_relay else recv_sem.at[j],
             device_id={"rows": target},
             device_id_type=MESH,
         )
@@ -285,32 +341,52 @@
     def leave(chosen, j):
         by_device(chosen, lambda leg: copy(leg, j).start(), 0)
 
-    def arrive(chosen, j):
-        by_device(chosen, lambda leg: copy(leg, j).wait_recv(), 1)
+    def hint_copy(flow):
+        k = hop_list.index(flow[1] - flow[0])
+        return pltpu.make_async_remote_copy(
+            src_ref=early.at[k],
+            dst_ref=hint.at[k],
+            send_sem=early_send.at[k],
+            recv_sem=early_recv.at[k],
+            device_id={"rows": flow[1]},
+            device_id_type=MESH,
+        )
 
     first_hop = [leg for leg in groups if not leg[2]]
-    second_hop = [leg for leg in groups if leg[2]]
-    to_relay = [leg for leg in groups if leg[3]]
-    to_owner = [leg for leg in groups if not leg[3]]
-
+    at_relay = [
+        (a, b)
+        for a in groups
+        for b in groups
+        if a[3] and b[2] and a[1] == b[0] and a[5] == b[4] and a[6] == b[6]
+    ]
+
+    for c in small:
+        c.wait()
     out_w[...] = send_weights(total, parts, me, block, send_rows, low_ref, weight_ref)
     sent_rows = sent.reshape(chunks, send_rows * SUB, LANES)
-    recv_rows = recv.reshape(chunks, slots * SUB, LANES)
 
     def prepare(j):
-        load(j).wait()
-        high, low_part = split(own[:, columns(j, WIDE)])
-        y = jnp.dot(
-            out_w[...],
-            jnp.concatenate([high, low_part, high], axis=0),
-            preferred_element_type=jnp.float32,
-        )
+        y = dot(out_w[...], triple(own[:, columns(j, WIDE)]))
         for b in range(SUB):
             sent_rows[j, pl.ds(b, send_rows, stride=SUB), :] = y[:, b * LANES : (b + 1) * LANES]
 
+    loads[0].wait()
     prepare(0)
     pl.semaphore_wait(barrier, table(me, waits))
     leave(first_hop, 0)
+
+    coarse_w[...] = coarse_weights(total, parts, me, block, low_ref, weight_ref)
+    last, known = chunks - 1, chunks - HINTED
+    eighth = block >> 3
+    loads[1].wait()
+    for h in range(HINTED):
+        y = pool_columns(dot(coarse_w[...], triple(own[:, columns(known + h, WIDE)])), 3)
+        at = pl.ds(h * (WIDE >> 3), WIDE >> 3)
+        for k in range(len(hop_list)):
+            early[k, :, at] = y[(k + 1) * eighth : (k + 2) * eighth]
+        for i in range(owners):
+            three[i, :, columns(known + h, WIDE >> 3)] = y[i * each : (i + 1) * each]
+    by_device(sorted(flows(total, parts)), lambda flow: hint_copy(flow).start(), 0)
 
     @pl.loop(1, chunks)
     def _(j):
@@ -320,65 +396,94 @@
     in_w[...] = own_weights(total, parts, me, block, slots, low_ref, weight_ref)
 
     def forward(j):
-        arrive(to_relay, j)
-        leave(second_hop, j)
+        def act(pair):
+            copy(pair[0], j).wait_recv()
+            copy(pair[1], j).start()
+
+        for i in range(parts):
+            mine = [pair for pair in at_relay if pair[1][0] == i]
+
+            if mine:
+                @pl.when(me == i)
+                def _():
+                    for pair in mine:
+                        act(pair)
+
+    def whole(ref, sem):
+        return pltpu.make_async_remote_copy(
+            src_ref=ref,
+            dst_ref=ref,
+            send_sem=sem,
+            recv_sem=sem,
+            device_id={"cols": lax.rem(col + 1, owners)},
+            device_id_type=MESH,
+        )
+
+    def arrive(j):
+        for i in range(parts):
+            if rows_in[i]:
+                @pl.when(me == i)
+                def _():
+                    whole(recv.at[j, pl.ds(0, rows_in[i])], recv_sem.at[j]).wait_recv()
 
     forward(0)
 
-    @pl.loop(0, chunks)
+    def compute(j, levels):
+        rows = chunk_rows(total, parts, j, own, recv, in_w, levels)
+        merc_ref[:, columns(j, WIDE)] = rows[0]
+        for level, ref in ((1, one_ref), (2, two_ref)):
+            ref[:, columns(j, WIDE >> level)] = pool_columns(rows[level], level)
+        if levels == 3:
+            pooled = pool_columns(rows[3], 3)
+            for i in range(owners):
+                three[i, :, columns(j, WIDE >> 3)] = pooled[i * each : (i + 1) * each]
+
+    @pl.loop(0, known)
     def _(j):
-        @pl.when(j + 1 < chunks)
-        def _():
-            forward(j + 1)
-
-        arrive(to_owner, j)
-        row = iota((slots, LANES), 0)
-        far = [
-            jnp.where(row < got, recv_rows[j, pl.ds(b, slots, stride=SUB), :], 0.0)
-            for b in range(SUB)
-        ]
-        x = jnp.concatenate([own[:, columns(j, WIDE)], jnp.concatenate(far, axis=1)], axis=0)
-        high, low_part = split(x)
-        y = jnp.dot(
-            in_w[...],
-            jnp.concatenate([high, low_part, high], axis=0),
-            preferred_element_type=jnp.float32,
-        )
-        merc_ref[:, columns(j, WIDE)] = y[:block]
-        at = block
-        for level, ref in ((1, one_ref), (2, two_ref)):
-            n = block >> level
-            ref[:, columns(j, WIDE >> level)] = pool_columns(y[at : at + n], level)
-            at += n
-        pooled = pool_columns(y[at:], 3)
-        each = three.shape[1]
+        forward(j + 1)
+        arrive(j)
+        compute(j, 3)
+
+    by_device(sorted(flows(total, parts)), lambda flow: hint_copy(flow).wait_recv(), 1)
+    for k, hop in enumerate(hop_list):
+        there = table(me, [int((i - hop, i) in flows(total, parts)) for i in range(parts)]) > 0
+        part = jnp.where(there, hint[k], 0.0)
         for i in range(owners):
-            three[i, :, columns(j, WIDE >> 3)] = pooled[i * each : (i + 1) * each]
-
-    shares = []
+            three[i, :, pl.ds(known * (WIDE >> 3), HINTED * (WIDE >> 3))] += part[i * each : (i + 1) * each]
+
     for i in range(1, owners):
         target = lax.rem(col + i, owners)
-        shares.append(
-            pltpu.make_async_remote_copy(
-                src_ref=three.at[target],
-                dst_ref=landed.at[owners - i],
-                send_sem=share_send.at[i],
-                recv_sem=share_recv.at[owners - i],
-                device_id={"cols": target},
-                device_id_type=MESH,
-            )
-        )
-    for c in shares:
-        c.start()
-
-    @pl.loop(0, chunks)
+        pltpu.make_async_remote_copy(
+            src_ref=three.at[target],
+            dst_ref=landed.at[owners - i],
+            send_sem=share_sem.at[0],
+            recv_sem=share_sem.at[1],
+            device_id={"cols": target},
+            device_id_type=MESH,
+        ).start()
+
+    @pl.loop(known, last)
     def _(j):
-        by_device(groups, lambda leg: copy(leg, j).wait_send(), 0)
+        forward(j + 1)
+        arrive(j)
+        compute(j, 2)
 
     landed[0] = three[col]
-    for c in shares:
-        c.wait()
+    others = landed.at[pl.ds(1, owners - 1)]
+    whole(others, share_sem.at[1]).wait_recv()
     finish(owners, col, landed, rows_ref, pooled_ref)
+    whole(others, share_sem.at[0]).wait_send()
+    by_device(sorted(flows(total, parts)), lambda flow: hint_copy(flow).wait_send(), 0)
+    arrive(last)
+    for i in range(parts):
+        held_rows = sum(leg[6] for leg in groups if leg[2] and leg[0] == i)
+
+        @pl.when(me == i)
+        def _():
+            if rows_out[i]:
+                whole(sent.at[:, pl.ds(0, rows_out[i])], send_sem.at[0]).wait_send()
+            if held_rows:
+                whole(held.at[:, pl.ds(0, held_rows)], send_sem.at[1]).wait_send()
 
 
 def finish(owners, col, landed, rows_ref, pooled_ref):
@@ -403,12 +508,29 @@
     )
 
 
-def write_kernel(*refs):
-    n = len(refs) // 2
-    sems = refs[2 * n]
-    copies = [pltpu.make_async_copy(refs[i], refs[n + i], sems.at[i]) for i in range(n)]
-    for c in copies:
-        c.start()
+def write_kernel(
+    total, parts,
+    merc_ref, one_ref, two_ref, rows_ref, pooled_ref, own, recv, in_w,
+    merc_out, one_out, two_out, rows_out, pooled_out,
+    merc_last, one_last, two_last, sems,
+):
+    last = own.shape[1] // WIDE - 1
+    copies = []
+
+    def put(src, dst):
+        copies.append(pltpu.make_async_copy(src, dst, sems.at[len(copies)]))
+        copies[-1].start()
+
+    levels = ((merc_ref, merc_out, merc_last), (one_ref, one_out, one_last), (two_ref, two_out, two_last))
+    for level, (ref, out, _) in enumerate(levels):
+        early = pl.ds(0, last * (WIDE >> level))
+        put(ref.at[:, early], out.at[:, early])
+    put(rows_ref, rows_out)
+    put(pooled_ref, pooled_out)
+    rows = chunk_rows(total, parts, last, own, recv, in_w, 2)
+    for level, (_, out, ref) in enumerate(levels):
+        ref[...] = pool_columns(rows[level], level) if level else rows[0]
+        put(ref, out.at[:, pl.ds(last * (WIDE >> level), WIDE >> level)])
     for c in copies:
         c.wait()
 
@@ -419,48 +541,60 @@
     _, _, sent, got = offsets(total, parts)
     send_rows, slots = up(max(sent), 16), up(max(got), 16)
     hold = max([n for by in relays(total, parts).values() for n in by.values()], default=1)
-    left = max([leg[7] + 1 for leg in legs(total, parts)], default=1)
-    come = max([leg[8] + 1 for leg in legs(total, parts)], default=1)
+    hops_out = len(all_hops(total, parts))
     chunks = width // WIDE
     each = (block >> 3) // owners
     wide_rows = block + block // 2 + block // 4 + block // 8
-    f32 = jnp.float32
+    f32, bf16 = jnp.float32, jnp.bfloat16
     shapes = [(block >> k, width >> k) for k in range(3)]
     shapes += [(each, owners * (width >> 3)), (each // 2, owners * (width >> 4))]
+    kept = [pltpu.VMEM(s, f32) for s in shapes]
+    kept += [
+        pltpu.VMEM((block, width), f32),
+        pltpu.VMEM((chunks, slots, SUB, LANES), f32),
+        pltpu.VMEM((wide_rows, 3 * (block + slots)), bf16),
+    ]
     vmem = pl.BlockSpec(memory_space=pltpu.VMEM)
     hbm = pl.BlockSpec(memory_space=pltpu.HBM)
+    dma = pltpu.SemaphoreType.DMA
     outs = pl.pallas_call(
         functools.partial(fused_kernel, total, parts, owners),
-        out_shape=[pltpu.VMEM(s, f32) for s in shapes],
-        in_specs=[vmem, vmem, hbm],
-        out_specs=[vmem] * len(shapes),
+        out_shape=kept,
+        in_specs=[hbm] * 3,
+        out_specs=[vmem] * len(kept),
         scratch_shapes=[
-            pltpu.VMEM((block, width), f32),
+            pltpu.VMEM((parts, block), jnp.int32),
+            pltpu.VMEM((parts, block), f32),
             pltpu.VMEM((chunks, send_rows, SUB, LANES), f32),
-            pltpu.VMEM((chunks, slots, SUB, LANES), f32),
             pltpu.VMEM((chunks, hold, SUB, LANES), f32),
             pltpu.VMEM((owners, each, width >> 3), f32),
             pltpu.VMEM((owners, each, width >> 3), f32),
-            pltpu.VMEM((send_rows, 3 * block), jnp.bfloat16),
-            pltpu.VMEM((wide_rows, 3 * (block + slots)), jnp.bfloat16),
-            pltpu.SemaphoreType.DMA((chunks,)),
-            pltpu.SemaphoreType.DMA((left, chunks)),
-            pltpu.SemaphoreType.DMA((come, chunks)),
-            pltpu.SemaphoreType.DMA((owners,)),
-            pltpu.SemaphoreType.DMA((owners,)),
+            pltpu.VMEM((send_rows, 3 * block), bf16),
+            pltpu.VMEM(((1 + hops_out) * (block >> 3), 3 * block), bf16),
+            pltpu.VMEM((hops_out, block >> 3, HINTED * (WIDE >> 3)), f32),
+            pltpu.VMEM((hops_out, block >> 3, HINTED * (WIDE >> 3)), f32),
+            dma((2,)),
+            dma((2,)),
+            dma((2,)),
+            dma((chunks,)),
+            dma((2, chunks)),
+            dma((hops_out,)),
+            dma((hops_out,)),
+            dma((2,)),
         ],
         compiler_params=pltpu.CompilerParams(
-            collective_id=0, has_side_effects=True, vmem_limit_bytes=54 << 20
+            collective_id=0, has_side_effects=True, vmem_limit_bytes=47 << 20
         ),
         name="reproject",
     )(low_row.reshape(parts, block), weight_low.reshape(parts, block), source)
     return pl.pallas_call(
-        write_kernel,
+        functools.partial(write_kernel, total, parts),
         out_shape=[jax.ShapeDtypeStruct(s, f32) for s in shapes],
-        in_specs=[vmem] * len(shapes),
+        in_specs=[vmem] * len(kept),
         out_specs=[hbm] * len(shapes),
-        scratch_shapes=[pltpu.SemaphoreType.DMA((len(shapes),))],
-        compiler_params=pltpu.CompilerParams(vmem_limit_bytes=8 << 20),
+        scratch_shapes=[pltpu.VMEM((block >> k, WIDE >> k), f32) for k in range(3)]
+        + [dma((len(shapes) + 3,))],
+        compiler_params=pltpu.CompilerParams(vmem_limit_bytes=24 << 20),
         name="write",
     )(*outs)
 

time: 69.8 us -> 64.8 us (0.928)
  Pallas kernels: 68.9 us -> 63.5 us
    pallas_call x1, Pallas kernels: 66.5 us -> 60.9 us  [body(): pl.pallas_call(functools.partial(fused_kernel, total, parts, owners), out...]
where the time goes in v3:
time: 64.8 us; the launch traced here: 64.1 us
  Pallas kernels  63.5 us (98%)
    pallas_call x1, Pallas kernels, body(): pl.pallas_call(functools.partial(fused_kernel, total, parts, owners), out...  60.9 us
    pallas_call x1, Pallas kernels, body(): pl.pallas_call(functools.partial(write_kernel, total, parts), out_shape=[...  2.53 us

profile of v3, /device:TPU:19, one launch (start us, length us, event | category | flops | bytes accessed | tf_op | source)
XLA Modules:
  0.0 64.1 jit_solution(6225071874537765058)
XLA Ops:
  0.6 60.9 %reproject.1 = (f32[128,8192]{1,0:T(8,128)S(1)}, f32[64,4096]{1,0:T(8,128)S(1)}, f32[32,2048]{1,0:T(8,128)S(1)}, f32[4,4096]{1,0:T(4,128)S(1)}, f32[2,2048]{1,0:...) custom-call(s32[8,128]{1,0:T(8,128)} %bitcast.2, ...), custom_call_target="tpu_custom_call" | custom-call | tf_op jit(solution)/shard_map/reproject/pallas_call | solution.py:560
  61.6 2.5 %write.1 = (f32[128,8192]{1,0:T(8,128)}, f32[64,4096]{1,0:T(8,128)}, f32[32,2048]{1,0:T(8,128)}, f32[4,4096]{1,0:T(4,128)}, f32[2,2048]{1,0:T(2,128)}) custom-call(f32[128,8192]{1,0:T(8,128)S(1)} %get-tuple-element.13.merc_ref, f32[64,4096]{1,0:T(8,128)S(1)} %get-tuple-element.14.one_ref, f32[32,2048]{1,0:T(8,128)S(1)} %get-tuple-element.15.two_ref, ...), custom_call_target="tpu_custom_call" | custom-call | tf_op jit(solution)/shard_map/write/pallas_call | solution.py:590

commit v4 on v3

--- a/solution.py
+++ b/solution.py
@@ -75,8 +75,9 @@
     plan, taken = {}, set()
     load = [moves.get((2 * z, 2 * z + 1), 0) for z in range(pairs)]
     across = 0.0
+    mean = sum(load) / pairs
     for z in range(pairs - 1):
-        across += load[z] - sum(load) / pairs
+        across += load[z] - mean
         n = int(round(abs(across)))
         at = z if across > 0 else z + 1
         key, relay = (2 * at, 2 * at + 1), 2 * at + (3 if across > 0 else -1)
@@ -87,7 +88,7 @@
     goal = sum(back) / pairs
     over = 0
     for z in range(pairs - 1):
-        want = int(round(goal * (0.9 if z == 0 else 1.0))) - over
+        want = int(round(goal * (0.975 if z == 0 else 1.0))) - over
         n = max(0, min(want, back[z]))
         if n and 2 * z not in taken:
             plan.setdefault((2 * z + 1, 2 * z + 2), {})[2 * z] = n
@@ -395,13 +396,15 @@
 
     in_w[...] = own_weights(total, parts, me, block, slots, low_ref, weight_ref)
 
-    def forward(j):
+    def forward(j, soon):
         def act(pair):
             copy(pair[0], j).wait_recv()
             copy(pair[1], j).start()
 
         for i in range(parts):
-            mine = [pair for pair in at_relay if pair[1][0] == i]
+            mine = [
+                (a, b) for a, b in at_relay if b[0] == i and (a[0] // 2 == b[1] // 2) == soon
+            ]
 
             if mine:
                 @pl.when(me == i)
@@ -426,7 +429,11 @@
                 def _():
                     whole(recv.at[j, pl.ds(0, rows_in[i])], recv_sem.at[j]).wait_recv()
 
-    forward(0)
+    @pl.loop(0, chunks)
+    def _(j):
+        forward(j, True)
+
+    forward(0, False)
 
     def compute(j, levels):
         rows = chunk_rows(total, parts, j, own, recv, in_w, levels)
@@ -440,7 +447,7 @@
 
     @pl.loop(0, known)
     def _(j):
-        forward(j + 1)
+        forward(j + 1, False)
         arrive(j)
         compute(j, 3)
 
@@ -464,7 +471,7 @@
 
     @pl.loop(known, last)
     def _(j):
-        forward(j + 1)
+        forward(j + 1, False)
         arrive(j)
         compute(j, 2)
 

time: 64.8 us -> 63.1 us (0.974)
  Pallas kernels: 63.5 us -> 62.2 us
    pallas_call x1, Pallas kernels: 60.9 us -> 59.7 us  [body(): pl.pallas_call(functools.partial(fused_kernel, total, parts, owners), out...]
where the time goes in v4:
time: 63.1 us; the launch traced here: 62.9 us
  Pallas kernels  62.2 us (99%)
  between operations  0.64 us (1%)
    pallas_call x1, Pallas kernels, body(): pl.pallas_call(functools.partial(fused_kernel, total, parts, owners), out...  59.7 us
    pallas_call x1, Pallas kernels, body(): pl.pallas_call(functools.partial(write_kernel, total, parts), out_shape=[...  2.53 us

profile of v4, /device:TPU:19, one launch (start us, length us, event | category | flops | bytes accessed | tf_op | source)
XLA Modules:
  0.0 62.9 jit_solution(18026398761424578206)
XLA Ops:
  0.6 59.7 %reproject.1 = (f32[128,8192]{1,0:T(8,128)S(1)}, f32[64,4096]{1,0:T(8,128)S(1)}, f32[32,2048]{1,0:T(8,128)S(1)}, f32[4,4096]{1,0:T(4,128)S(1)}, f32[2,2048]{1,0:...) custom-call(s32[8,128]{1,0:T(8,128)} %bitcast.2, ...), custom_call_target="tpu_custom_call" | custom-call | tf_op jit(solution)/shard_map/reproject/pallas_call | solution.py:567
  60.3 2.5 %write.1 = (f32[128,8192]{1,0:T(8,128)}, f32[64,4096]{1,0:T(8,128)}, f32[32,2048]{1,0:T(8,128)}, f32[4,4096]{1,0:T(4,128)}, f32[2,2048]{1,0:T(2,128)}) custom-call(f32[128,8192]{1,0:T(8,128)S(1)} %get-tuple-element.13.merc_ref, f32[64,4096]{1,0:T(8,128)S(1)} %get-tuple-element.14.one_ref, f32[32,2048]{1,0:T(8,128)S(1)} %get-tuple-element.15.two_ref, ...), custom_call_target="tpu_custom_call" | custom-call | tf_op jit(solution)/shard_map/write/pallas_call | solution.py:597

commit v5 on v4

--- a/solution.py
+++ b/solution.py
@@ -99,6 +99,10 @@
     return plan
 
 
+def near(i, j):
+    return i // 2 == j // 2 or abs(i - j) == 2
+
+
 def halves(n):
     return [(0, n // 2), (n // 2, n - n // 2)] if n > 1 else [(0, n)]
 
@@ -176,11 +180,12 @@
 
 def send_weights(total, parts, me, block, rows, low_ref, weight_ref):
     k, c = iota((rows, block), 0), iota((rows, block), 1)
-    out = jnp.zeros((rows, block), jnp.float32)
+    high = jnp.zeros((rows, block), jnp.float32)
+    low_part = high
     for delta in hops(total, parts, False):
         n, at, first = flow_tables(total, parts, me, delta, False, True)
         here = (k >= at) & (k < at + n)
-        out = out + jnp.where(here & (c == k - at + first - me * block), 1.0, 0.0)
+        high = high + jnp.where(here & (c == k - at + first - me * block), 1.0, 0.0)
     for delta in hops(total, parts, True):
         n, at, first = flow_tables(total, parts, me, delta, True, True)
         owner = jnp.clip(me + delta, 0, parts - 1)
@@ -189,8 +194,14 @@
         row = iota((block, block), 0)
         band = jnp.where(row == low, weight, 0.0) + jnp.where(row == low + 1, 1.0 - weight, 0.0)
         pick = (k >= at) & (k < at + n) & (c == k - at + first - owner * block)
-        out = out + exact_dot(jnp.where(pick, 1.0, 0.0), band)
-    high, low_part = split(out)
+        both = lax.dot_general(
+            jnp.where(pick, 1.0, 0.0).astype(jnp.bfloat16),
+            jnp.concatenate(split(band), axis=0),
+            (((1,), (1,)), ((), ())),
+            preferred_element_type=jnp.float32,
+        )
+        high, low_part = high + both[:, :block], low_part + both[:, block:]
+    high, low_part = high.astype(jnp.bfloat16), low_part.astype(jnp.bfloat16)
     return jnp.concatenate([high, high, low_part], axis=1)
 
 
@@ -253,21 +264,23 @@
     return jnp.dot(a, b, preferred_element_type=jnp.float32)
 
 
-def chunk_rows(total, parts, j, own, recv, in_w, levels):
-    block, (chunks, slots) = own.shape[0], recv.shape[:2]
+def chunk_operand(total, parts, j, own, recv):
+    chunks, slots = recv.shape[:2]
     got = table(lax.axis_index("rows"), offsets(total, parts)[3])
     rows = recv.reshape(chunks, slots * SUB, LANES)
     row = iota((slots, LANES), 0)
     far = [
         jnp.where(row < got, rows[j, pl.ds(b, slots, stride=SUB), :], 0.0) for b in range(SUB)
     ]
-    x = jnp.concatenate([own[:, columns(j, WIDE)], jnp.concatenate(far, axis=1)], axis=0)
-    y = dot(in_w[: 2 * block - (block >> levels), :], triple(x))
-    out, at = [], 0
-    for level in range(levels + 1):
-        out.append(y[at : at + (block >> level)])
-        at += block >> level
-    return out
+    return triple(
+        jnp.concatenate([own[:, columns(j, WIDE)], jnp.concatenate(far, axis=1)], axis=0)
+    )
+
+
+def chunk_rows(block, in_w, x, levels):
+    at = [2 * block - (2 * block >> level) for level in levels]
+    y = dot(in_w[at[0] : at[-1] + (block >> levels[-1]), :], x)
+    return [y[a - at[0] : a - at[0] + (block >> level)] for a, level in zip(at, levels)]
 
 
 def fused_kernel(
@@ -275,7 +288,7 @@
     low_hbm, weight_hbm, source_ref,
     merc_ref, one_ref, two_ref, rows_ref, pooled_ref, own, recv, in_w,
     low_ref, weight_ref, sent, held, three, landed, out_w, coarse_w, early, hint,
-    small_sem, own_sem, send_sem, recv_sem, held_sem, early_send, early_recv, share_sem,
+    small_sem, own_sem, send_sem, recv_sem, held_sem, early_send, early_recv, share_sem, met_sem,
 ):
     block, width = source_ref.shape
     chunks = width // WIDE
@@ -287,6 +300,26 @@
     each = three.shape[1]
     hop_list = all_hops(total, parts)
 
+    barrier = pltpu.get_barrier_semaphore()
+    ties = {leg[:2] for leg in groups} | set(flows(total, parts))
+    met = [[j for j in range(parts) if (i, j) in ties or (j, i) in ties] for i in range(parts)]
+    stepped = bool(relays(total, parts))
+    if stepped:
+        met = [[j for j in range(parts) if j != i and near(i, j)] for i in range(parts)]
+
+    def greet(sem):
+        for i in range(parts):
+            @pl.when(me == i)
+            def _():
+                for j in met[i]:
+                    pl.semaphore_signal(sem, inc=1, device_id={"rows": j}, device_id_type=MESH)
+
+    greet(barrier)
+    for i in range(1, owners):
+        pl.semaphore_signal(
+            barrier, inc=1, device_id={"cols": lax.rem(col + i, owners)}, device_id_type=MESH
+        )
+
     loads = [
         pltpu.make_async_copy(source_ref.at[:, at], own.at[:, at], own_sem.at[i])
         for i, at in enumerate((pl.ds(0, WIDE), pl.ds(WIDE, width - WIDE)))
@@ -309,21 +342,6 @@
                 def _():
                     for leg in mine:
                         act(leg)
-
-    barrier = pltpu.get_barrier_semaphore()
-    ties = [leg[:2] for leg in groups] + list(flows(total, parts))
-    met = [sorted({a[1 - k] for a in ties for k in (0, 1) if a[k] == i}) for i in range(parts)]
-    for i in range(parts):
-        @pl.when(me == i)
-        def _():
-            for other in met[i]:
-                pl.semaphore_signal(barrier, inc=1, device_id={"rows": other}, device_id_type=MESH)
-
-    for i in range(1, owners):
-        pl.semaphore_signal(
-            barrier, inc=1, device_id={"cols": lax.rem(col + i, owners)}, device_id_type=MESH
-        )
-    waits = [len(met[i]) + owners - 1 for i in range(parts)]
 
     loads[1].start()
 
@@ -373,8 +391,11 @@
 
     loads[0].wait()
     prepare(0)
-    pl.semaphore_wait(barrier, table(me, waits))
-    leave(first_hop, 0)
+    pl.semaphore_wait(barrier, table(me, [len(m) + owners - 1 for m in met]))
+    if stepped:
+        greet(met_sem)
+    here = [leg for leg in first_hop if not stepped or near(*leg[:2])]
+    leave(here, 0)
 
     coarse_w[...] = coarse_weights(total, parts, me, block, low_ref, weight_ref)
     last, known = chunks - 1, chunks - HINTED
@@ -382,11 +403,13 @@
     loads[1].wait()
     for h in range(HINTED):
         y = pool_columns(dot(coarse_w[...], triple(own[:, columns(known + h, WIDE)])), 3)
-        at = pl.ds(h * (WIDE >> 3), WIDE >> 3)
         for k in range(len(hop_list)):
-            early[k, :, at] = y[(k + 1) * eighth : (k + 2) * eighth]
+            early[k, :, columns(h, WIDE >> 3)] = y[(k + 1) * eighth : (k + 2) * eighth]
         for i in range(owners):
             three[i, :, columns(known + h, WIDE >> 3)] = y[i * each : (i + 1) * each]
+    if stepped:
+        pl.semaphore_wait(met_sem, table(me, [len(m) for m in met]))
+        leave([leg for leg in first_hop if leg not in here], 0)
     by_device(sorted(flows(total, parts)), lambda flow: hint_copy(flow).start(), 0)
 
     @pl.loop(1, chunks)
@@ -435,21 +458,27 @@
 
     forward(0, False)
 
-    def compute(j, levels):
-        rows = chunk_rows(total, parts, j, own, recv, in_w, levels)
+    def compute(x, j):
+        rows = chunk_rows(block, in_w, x, (0, 1, 2))
         merc_ref[:, columns(j, WIDE)] = rows[0]
         for level, ref in ((1, one_ref), (2, two_ref)):
             ref[:, columns(j, WIDE >> level)] = pool_columns(rows[level], level)
-        if levels == 3:
-            pooled = pool_columns(rows[3], 3)
-            for i in range(owners):
-                three[i, :, columns(j, WIDE >> 3)] = pooled[i * each : (i + 1) * each]
-
-    @pl.loop(0, known)
-    def _(j):
+
+    def coarse(x, j):
+        pooled = pool_columns(chunk_rows(block, in_w, x, (3,))[0], 3)
+        for i in range(owners):
+            three[i, :, columns(j, WIDE >> 3)] = pooled[i * each : (i + 1) * each]
+
+    def receive(j):
         forward(j + 1, False)
         arrive(j)
-        compute(j, 3)
+        return chunk_operand(total, parts, j, own, recv)
+
+    @pl.loop(0, known - 1)
+    def _(j):
+        x = receive(j)
+        compute(x, j)
+        coarse(x, j)
 
     by_device(sorted(flows(total, parts)), lambda flow: hint_copy(flow).wait_recv(), 1)
     for k, hop in enumerate(hop_list):
@@ -458,6 +487,8 @@
         for i in range(owners):
             three[i, :, pl.ds(known * (WIDE >> 3), HINTED * (WIDE >> 3))] += part[i * each : (i + 1) * each]
 
+    x = receive(known - 1)
+    coarse(x, known - 1)
     for i in range(1, owners):
         target = lax.rem(col + i, owners)
         pltpu.make_async_remote_copy(
@@ -468,12 +499,11 @@
             device_id={"cols": target},
             device_id_type=MESH,
         ).start()
+    compute(x, known - 1)
 
     @pl.loop(known, last)
     def _(j):
-        forward(j + 1, False)
-        arrive(j)
-        compute(j, 2)
+        compute(receive(j), j)
 
     landed[0] = three[col]
     others = landed.at[pl.ds(1, owners - 1)]
@@ -534,7 +564,8 @@
         put(ref.at[:, early], out.at[:, early])
     put(rows_ref, rows_out)
     put(pooled_ref, pooled_out)
-    rows = chunk_rows(total, parts, last, own, recv, in_w, 2)
+    x = chunk_operand(total, parts, last, own, recv)
+    rows = chunk_rows(own.shape[0], in_w, x, (0, 1, 2))
     for level, (_, out, ref) in enumerate(levels):
         ref[...] = pool_columns(rows[level], level) if level else rows[0]
         put(ref, out.at[:, pl.ds(last * (WIDE >> level), WIDE >> level)])
@@ -588,6 +619,7 @@
             dma((hops_out,)),
             dma((hops_out,)),
             dma((2,)),
+            pltpu.SemaphoreType.REGULAR,
         ],
         compiler_params=pltpu.CompilerParams(
             collective_id=0, has_side_effects=True, vmem_limit_bytes=47 << 20

time: 63.1 us -> 63.1 us (level); the launches traced: 62.9 us -> 62.2 us
  Pallas kernels: 62.2 us -> 61.5 us
    pallas_call x1, Pallas kernels: 59.7 us -> 59 us  [body(): pl.pallas_call(functools.partial(fused_kernel, total, parts, owners), out...]
where the time goes in v5:
time: 63.1 us; the launch traced here: 62.2 us
  Pallas kernels  61.5 us (97%)
  between operations  0.64 us (1%)
    pallas_call x1, Pallas kernels, body(): pl.pallas_call(functools.partial(fused_kernel, total, parts, owners), out...  59 us
    pallas_call x1, Pallas kernels, body(): pl.pallas_call(functools.partial(write_kernel, total, parts), out_shape=[...  2.53 us

profile of v5, /device:TPU:19, one launch (start us, length us, event | category | flops | bytes accessed | tf_op | source)
XLA Modules:
  0.0 62.2 jit_solution(17560318270018181156)
XLA Ops:
  0.6 59.0 %reproject.1 = (f32[128,8192]{1,0:T(8,128)S(1)}, f32[64,4096]{1,0:T(8,128)S(1)}, f32[32,2048]{1,0:T(8,128)S(1)}, f32[4,4096]{1,0:T(4,128)S(1)}, f32[2,2048]{1,0:...) custom-call(s32[8,128]{1,0:T(8,128)} %bitcast.2, ...), custom_call_target="tpu_custom_call" | custom-call | tf_op jit(solution)/shard_map/reproject/pallas_call | solution.py:598
  59.6 2.5 %write.1 = (f32[128,8192]{1,0:T(8,128)}, f32[64,4096]{1,0:T(8,128)}, f32[32,2048]{1,0:T(8,128)}, f32[4,4096]{1,0:T(4,128)}, f32[2,2048]{1,0:T(2,128)}) custom-call(f32[128,8192]{1,0:T(8,128)S(1)} %get-tuple-element.13.merc_ref, f32[64,4096]{1,0:T(8,128)S(1)} %get-tuple-element.14.one_ref, f32[32,2048]{1,0:T(8,128)S(1)} %get-tuple-element.15.two_ref, ...), custom_call_target="tpu_custom_call" | custom-call | tf_op jit(solution)/shard_map/write/pallas_call | solution.py:629

commit v6 on v5

--- a/solution.py
+++ b/solution.py
@@ -14,6 +14,7 @@
 WIDE = SUB * LANES
 JITTER = 2
 HINTED = 2
+PIECES = 2
 MESH = pl.DeviceIdType.MESH
 
 
@@ -345,6 +346,13 @@
 
     loads[1].start()
 
+    def send(leg, j):
+        s, d, relayed, to_relay, at, to, n, half = leg
+        cuts = [n * i // PIECES for i in range(PIECES + 1)]
+        for low, high in zip(cuts, cuts[1:]):
+            if high > low:
+                copy((s, d, relayed, to_relay, at + low, to + low, high - low, half), j).start()
+
     def copy(leg, j):
         _, target, relayed, to_relay, at, to, n, half = leg
         src, dst = (held if relayed else sent), (held if to_relay else recv)
@@ -358,7 +366,7 @@
         )
 
     def leave(chosen, j):
-        by_device(chosen, lambda leg: copy(leg, j).start(), 0)
+        by_device(chosen, lambda leg: send(leg, j), 0)
 
     def hint_copy(flow):
         k = hop_list.index(flow[1] - flow[0])
@@ -422,7 +430,7 @@
     def forward(j, soon):
         def act(pair):
             copy(pair[0], j).wait_recv()
-            copy(pair[1], j).start()
+            send(pair[1], j)
 
         for i in range(parts):
             mine = [

time: 63.1 us -> 63.1 us (level)
  no operation moved by 1% of the time
where the time goes in v6:
time: 63.1 us; the launch traced here: 62.1 us
  Pallas kernels  61.5 us (97%)
  between operations  0.64 us (1%)
    pallas_call x1, Pallas kernels, body(): pl.pallas_call(functools.partial(fused_kernel, total, parts, owners), out...  59 us
    pallas_call x1, Pallas kernels, body(): pl.pallas_call(functools.partial(write_kernel, total, parts), out_shape=[...  2.53 us

profile of v6, /device:TPU:19, one launch (start us, length us, event | category | flops | bytes accessed | tf_op | source)
XLA Modules:
  0.0 62.1 jit_solution(15334684459624264299)
XLA Ops:
  0.6 59.0 %reproject.1 = (f32[128,8192]{1,0:T(8,128)S(1)}, f32[64,4096]{1,0:T(8,128)S(1)}, f32[32,2048]{1,0:T(8,128)S(1)}, f32[4,4096]{1,0:T(4,128)S(1)}, f32[2,2048]{1,0:...) custom-call(s32[8,128]{1,0:T(8,128)} %bitcast.2, ...), custom_call_target="tpu_custom_call" | custom-call | tf_op jit(solution)/shard_map/reproject/pallas_call | solution.py:606
  59.6 2.5 %write.1 = (f32[128,8192]{1,0:T(8,128)}, f32[64,4096]{1,0:T(8,128)}, f32[32,2048]{1,0:T(8,128)}, f32[4,4096]{1,0:T(4,128)}, f32[2,2048]{1,0:T(2,128)}) custom-call(f32[128,8192]{1,0:T(8,128)S(1)} %get-tuple-element.13.merc_ref, f32[64,4096]{1,0:T(8,128)S(1)} %get-tuple-element.14.one_ref, f32[32,2048]{1,0:T(8,128)S(1)} %get-tuple-element.15.two_ref, ...), custom_call_target="tpu_custom_call" | custom-call | tf_op jit(solution)/shard_map/write/pallas_call | solution.py:637

commit v7 on v5

--- a/solution.py
+++ b/solution.py
@@ -392,10 +392,10 @@
     loads[0].wait()
     prepare(0)
     pl.semaphore_wait(barrier, table(me, [len(m) + owners - 1 for m in met]))
+    here = [leg for leg in first_hop if not stepped or near(*leg[:2])]
+    leave(here, 0)
     if stepped:
         greet(met_sem)
-    here = [leg for leg in first_hop if not stepped or near(*leg[:2])]
-    leave(here, 0)
 
     coarse_w[...] = coarse_weights(total, parts, me, block, low_ref, weight_ref)
     last, known = chunks - 1, chunks - HINTED

time: 63.1 us -> 63.1 us (level)
  no operation moved by 1% of the time
where the time goes in v7:
time: 63.1 us; the launch traced here: 62.2 us
  Pallas kernels  61.5 us (97%)
  between operations  0.64 us (1%)
    pallas_call x1, Pallas kernels, body(): pl.pallas_call(functools.partial(fused_kernel, total, parts, owners), out...  59 us
    pallas_call x1, Pallas kernels, body(): pl.pallas_call(functools.partial(write_kernel, total, parts), out_shape=[...  2.53 us

profile of v7, /device:TPU:19, one launch (start us, length us, event | category | flops | bytes accessed | tf_op | source)
XLA Modules:
  0.0 62.2 jit_solution(10835621919472610360)
XLA Ops:
  0.6 59.0 %reproject.1 = (f32[128,8192]{1,0:T(8,128)S(1)}, f32[64,4096]{1,0:T(8,128)S(1)}, f32[32,2048]{1,0:T(8,128)S(1)}, f32[4,4096]{1,0:T(4,128)S(1)}, f32[2,2048]{1,0:...) custom-call(s32[8,128]{1,0:T(8,128)} %bitcast.2, ...), custom_call_target="tpu_custom_call" | custom-call | tf_op jit(solution)/shard_map/reproject/pallas_call | solution.py:598
  59.6 2.5 %write.1 = (f32[128,8192]{1,0:T(8,128)}, f32[64,4096]{1,0:T(8,128)}, f32[32,2048]{1,0:T(8,128)}, f32[4,4096]{1,0:T(4,128)}, f32[2,2048]{1,0:T(2,128)}) custom-call(f32[128,8192]{1,0:T(8,128)S(1)} %get-tuple-element.13.merc_ref, f32[64,4096]{1,0:T(8,128)S(1)} %get-tuple-element.14.one_ref, f32[32,2048]{1,0:T(8,128)S(1)} %get-tuple-element.15.two_ref, ...), custom_call_target="tpu_custom_call" | custom-call | tf_op jit(solution)/shard_map/write/pallas_call | solution.py:629

commit v8 on v7

--- a/solution.py
+++ b/solution.py
@@ -288,7 +288,7 @@
     low_hbm, weight_hbm, source_ref,
     merc_ref, one_ref, two_ref, rows_ref, pooled_ref, own, recv, in_w,
     low_ref, weight_ref, sent, held, three, landed, out_w, coarse_w, early, hint,
-    small_sem, own_sem, send_sem, recv_sem, held_sem, early_send, early_recv, share_sem, met_sem,
+    small_sem, own_sem, send_sem, recv_sem, held_sem, early_sem, share_sem, met_sem,
 ):
     block, width = source_ref.shape
     chunks = width // WIDE
@@ -365,8 +365,8 @@
         return pltpu.make_async_remote_copy(
             src_ref=early.at[k],
             dst_ref=hint.at[k],
-            send_sem=early_send.at[k],
-            recv_sem=early_recv.at[k],
+            send_sem=early_sem.at[0],
+            recv_sem=early_sem.at[1],
             device_id={"rows": flow[1]},
             device_id_type=MESH,
         )
@@ -480,7 +480,13 @@
         compute(x, j)
         coarse(x, j)
 
-    by_device(sorted(flows(total, parts)), lambda flow: hint_copy(flow).wait_recv(), 1)
+    for i in range(parts):
+        count = sum(d == i for _, d in flows(total, parts))
+        if count:
+            @pl.when(me == i)
+            def _():
+                whole(hint.at[pl.ds(0, count)], early_sem.at[1]).wait_recv()
+
     for k, hop in enumerate(hop_list):
         there = table(me, [int((i - hop, i) in flows(total, parts)) for i in range(parts)]) > 0
         part = jnp.where(there, hint[k], 0.0)
@@ -510,13 +516,15 @@
     whole(others, share_sem.at[1]).wait_recv()
     finish(owners, col, landed, rows_ref, pooled_ref)
     whole(others, share_sem.at[0]).wait_send()
-    by_device(sorted(flows(total, parts)), lambda flow: hint_copy(flow).wait_send(), 0)
     arrive(last)
     for i in range(parts):
         held_rows = sum(leg[6] for leg in groups if leg[2] and leg[0] == i)
+        count = sum(a == i for a, _ in flows(total, parts))
 
         @pl.when(me == i)
         def _():
+            if count:
+                whole(early.at[pl.ds(0, count)], early_sem.at[0]).wait_send()
             if rows_out[i]:
                 whole(sent.at[:, pl.ds(0, rows_out[i])], send_sem.at[0]).wait_send()
             if held_rows:
@@ -616,8 +624,7 @@
             dma((2,)),
             dma((chunks,)),
             dma((2, chunks)),
-            dma((hops_out,)),
-            dma((hops_out,)),
+            dma((2,)),
             dma((2,)),
             pltpu.SemaphoreType.REGULAR,
         ],

time: 63.1 us -> 63.1 us (level)
  no operation moved by 1% of the time
where the time goes in v8:
time: 63.1 us; the launch traced here: 62.1 us
  Pallas kernels  61.5 us (97%)
  between operations  0.64 us (1%)
    pallas_call x1, Pallas kernels, body(): pl.pallas_call(functools.partial(fused_kernel, total, parts, owners), out...  59 us
    pallas_call x1, Pallas kernels, body(): pl.pallas_call(functools.partial(write_kernel, total, parts), out_shape=[...  2.53 us

profile of v8, /device:TPU:19, one launch (start us, length us, event | category | flops | bytes accessed | tf_op | source)
XLA Modules:
  0.0 62.1 jit_solution(6324671355601102148)
XLA Ops:
  0.6 59.0 %reproject.1 = (f32[128,8192]{1,0:T(8,128)S(1)}, f32[64,4096]{1,0:T(8,128)S(1)}, f32[32,2048]{1,0:T(8,128)S(1)}, f32[4,4096]{1,0:T(4,128)S(1)}, f32[2,2048]{1,0:...) custom-call(s32[8,128]{1,0:T(8,128)} %bitcast.2, ...), custom_call_target="tpu_custom_call" | custom-call | tf_op jit(solution)/shard_map/reproject/pallas_call | solution.py:606
  59.6 2.5 %write.1 = (f32[128,8192]{1,0:T(8,128)}, f32[64,4096]{1,0:T(8,128)}, f32[32,2048]{1,0:T(8,128)}, f32[4,4096]{1,0:T(4,128)}, f32[2,2048]{1,0:T(2,128)}) custom-call(f32[128,8192]{1,0:T(8,128)S(1)} %get-tuple-element.13.merc_ref, f32[64,4096]{1,0:T(8,128)S(1)} %get-tuple-element.14.one_ref, f32[32,2048]{1,0:T(8,128)S(1)} %get-tuple-element.15.two_ref, ...), custom_call_target="tpu_custom_call" | custom-call | tf_op jit(solution)/shard_map/write/pallas_call | solution.py:636
